TPU v7x, 512 devices: a 8x2x16 block of a 8x8x16 slice. The times are simulated.
512 devices in a mesh: groups: 2 (over y), dp: 16 (over z), head: 8 (over x), sub: 2 (over core).
Axes of the slice: x: 8, y: 2, z: 16, core: 2. Of those that a mesh axis runs over, the one named last changes fastest.
The devices are a block of a 8x8x16 slice.
Arguments:
- queries: bfloat16 [512, 64, 128], P(('groups', 'dp', 'sub'), 'head'), parts along dimension 0, may hold values from -8 to 8
- kv_cache: bfloat16 [32768, 8, 2, 16, 128], P(('groups', 'dp', 'sub'), 'head'), parts along dimension 0, may hold values from -8 to 8
- keep: int32 [512, 48], P(('groups', 'dp', 'sub')), parts along dimension 0, may hold values from 0 to 63, as said below
- lengths: int32 [512], P(('groups', 'dp', 'sub')), parts along dimension 0, may hold values from 384 to 768
- placement: int32 [512, 64], P(('groups', 'dp', 'sub')), parts along dimension 0, may hold values from 0 to 16383, as said below
- positions: int32 [512], P(('groups', 'dp', 'sub')), parts along dimension 0, may hold values from 0 to 4095
Outputs:
- attention: bfloat16 [512, 64, 128], P(('groups', 'dp', 'sub'), 'head'), parts along dimension 0
- log_norm: float32 [512, 64], P(('groups', 'dp', 'sub'), 'head'), parts along dimension 0
There are 2 independent parts, one for each index of `groups`. A program takes and returns all parts, laid end to end along the dimension named above; each array names one. Nothing has to cross between parts.
Inputs may be any that keep to these rules, and one draw needn't show every extreme that they name: `keep`: each row holds distinct block numbers in increasing order. `placement`: every cache row is named once; the 8 requests of one device (aligned groups of 8 rows) have exactly 16 of their blocks in the cache rows of each device.
All inputs are finite; a program needn't handle non-finite values.
Results may differ from a plain program's by a relative error of at most 0.0058.
Values may be sent and summed in bfloat16 or wider, within the bound.
No kernel may reach another device: no remote copies, remote signals or barrier semaphores. Data moves between devices by JAX's collectives and lax.ppermute only.
A program may use at most 64 MiB of HBM per device.

v0:
```python
from functools import partial

import jax
import jax.numpy as jnp
from jax import lax
from jax.sharding import PartitionSpec as P


def side_by_side(arrays, axis, split_dim, concat_dim, along):
    ends, at = ([], 0)
    for a in arrays[:-1]:
        at += a.shape[along]
        ends.append(at)
    both = jnp.concatenate(arrays, axis=along)
    return tuple(
        jnp.split(
            lax.all_to_all(both, axis, split_axis=split_dim, concat_axis=concat_dim, tiled=True),
            ends,
            axis=along,
        )
    )


def in_order(parts, dim):
    parts = jnp.moveaxis(parts, 0, dim)
    lengths = parts.shape
    return parts.reshape(*lengths[:dim], lengths[dim] * lengths[dim + 1], *lengths[dim + 2 :])


def from_everyone(value, axis):
    size = lax.axis_size(axis)
    return lax.all_to_all(
        jnp.broadcast_to(value[None], (size, *value.shape)), axis, 0, 0, tiled=True
    )


def gather_directly(value, axis, dim):
    return in_order(from_everyone(value, axis), dim)


def rotate(values, positions):
    half = values.shape[-1] // 2
    inverse = 1000000.0 ** (-(2.0 * jnp.arange(half, dtype=jnp.float32)) / values.shape[-1])
    angle = positions.astype(jnp.float32)[:, None] * inverse[None, :]
    cosine = jnp.cos(angle)[:, None, :]
    sine = jnp.sin(angle)[:, None, :]
    first = values[..., :half]
    second = values[..., half:]
    return jnp.concatenate(
        [first * cosine - second * sine, second * cosine + first * sine], axis=-1
    )


def select_rows(row_ids, kv_cache):
    pool_dev = kv_cache.shape[0]
    onehot = (row_ids[:, None] == jnp.arange(pool_dev, dtype=jnp.int32)[None, :]).astype(
        jnp.bfloat16
    )
    picked = jnp.dot(onehot, kv_cache.reshape(pool_dev, -1), preferred_element_type=jnp.float32)
    return picked.astype(jnp.bfloat16).reshape((row_ids.shape[0],) + kv_cache.shape[1:])


def block_partial(selected, blocks, counts):
    factor = selected.shape[-1] ** (-0.5)
    scores = (
        jnp.einsum("skgd,sktd->skgt", selected, blocks[:, :, 0], preferred_element_type=jnp.float32)
        * factor
    )
    live = (jnp.arange(blocks.shape[3], dtype=jnp.int32)[None, :] < counts[:, None])[
        :, None, None, :
    ]
    peak = jnp.max(jnp.where(live, scores, -1e30), axis=-1)
    weights = jnp.where(live, jnp.exp(scores - peak[..., None]), 0.0).astype(jnp.bfloat16)
    totals = jnp.sum(weights.astype(jnp.float32), axis=-1)
    outputs = jnp.einsum(
        "skgt,sktd->skgd", weights, blocks[:, :, 1], preferred_element_type=jnp.float32
    )
    return (peak, totals, outputs)


def combine_slots(peak, totals, outputs, request, requests):
    member = request[None, :] == jnp.arange(requests, dtype=jnp.int32)[:, None]
    inside = member[:, :, None, None]
    top = jnp.max(jnp.where(inside, peak[None], -1e30), axis=1)
    scale = jnp.where(inside, jnp.exp(peak[None] - top[:, None]), 0.0)
    norm = jnp.sum(scale * totals[None], axis=1)
    merged = jnp.einsum("rmkg,mkgd->rkgd", scale, outputs, precision=lax.Precision.HIGHEST)
    return (top, norm, merged)


def local(queries, kv_cache, keep, lengths, placement, positions):
    owners = lax.axis_size(("dp", "sub"))
    requests, q_heads, head_dim = queries.shape
    pool_dev, kv_heads, _, block_len, _ = kv_cache.shape
    spread = pool_dev // owners
    group = q_heads // kv_heads
    kept = keep.shape[1]
    rotated = rotate(queries.astype(jnp.float32), positions).astype(jnp.bfloat16)
    rotated = rotated.reshape(requests, kv_heads, group, head_dim)
    cache_rows = jnp.take_along_axis(placement, keep, axis=1)
    live_counts = jnp.clip(
        lengths[:, None] - jnp.arange(kept, dtype=jnp.int32)[None, :] * block_len, 0, block_len
    )
    owner_of = (cache_rows // pool_dev).reshape(-1)
    local_of = (cache_rows % pool_dev).reshape(-1)
    count_of = live_counts.reshape(-1)
    request_of = jnp.repeat(jnp.arange(requests, dtype=jnp.int32), kept)
    live = count_of > 0
    member = (owner_of[:, None] == jnp.arange(owners, dtype=jnp.int32)[None, :]) & live[:, None]
    running = jnp.cumsum(member.astype(jnp.int32), axis=0) - 1
    ranks = jnp.sum(jnp.where(member, running, 0), axis=1)
    target = jnp.where(live, owner_of * spread + ranks, owners * spread)
    send_ids = jnp.full((owners * spread,), -1, jnp.int32).at[target].set(local_of, mode="drop")
    send_meta = (
        jnp.zeros((owners * spread,), jnp.int32)
        .at[target]
        .set(request_of * (block_len + 1) + count_of, mode="drop")
    )
    send_ids = send_ids.reshape(owners, spread)
    send_meta = send_meta.reshape(owners, spread)
    got_ids, got_meta = side_by_side((send_ids, send_meta), ("dp", "sub"), 0, 0, 1)
    everyone = gather_directly(rotated, ("dp", "sub"), 0)
    picked = select_rows(got_ids.reshape(-1), kv_cache)
    slot_request = got_meta // (block_len + 1)
    slot_count = (got_meta % (block_len + 1)).reshape(-1)
    source = (jnp.arange(owners, dtype=jnp.int32)[:, None] * requests + slot_request).reshape(-1)
    selected = jnp.take(everyone, source, axis=0)
    peak, totals, outputs = block_partial(selected, picked, slot_count)
    peak = peak.reshape((owners, spread) + peak.shape[1:])
    totals = totals.reshape((owners, spread) + totals.shape[1:])
    outputs = outputs.reshape((owners, spread) + outputs.shape[1:])
    per_source = jax.vmap(partial(combine_slots, requests=requests))
    part_top, part_norm, part_merged = per_source(peak, totals, outputs, slot_request)
    back_top, back_norm, back_merged = (
        lax.all_to_all(part_top, ("dp", "sub"), split_axis=0, concat_axis=0, tiled=True),
        lax.all_to_all(part_norm, ("dp", "sub"), split_axis=0, concat_axis=0, tiled=True),
        lax.all_to_all(part_merged, ("dp", "sub"), split_axis=0, concat_axis=0, tiled=True),
    )
    top = jnp.max(back_top, axis=0)
    scale = jnp.exp(back_top - top[None])
    norm = jnp.sum(scale * back_norm, axis=0)
    merged = jnp.sum(scale[..., None] * back_merged, axis=0)
    attention = (merged / norm[..., None]).reshape(requests, q_heads, head_dim).astype(jnp.bfloat16)
    log_norm = (top + jnp.log(norm)).reshape(requests, q_heads)
    return (attention, log_norm)


def solution(mesh):
    in_specs = (
        P(("groups", "dp", "sub"), "head", None),
        P(("groups", "dp", "sub"), "head", None, None, None),
        P(("groups", "dp", "sub"), None),
        P(("groups", "dp", "sub")),
        P(("groups", "dp", "sub"), None),
        P(("groups", "dp", "sub")),
    )
    out_specs = (P(("groups", "dp", "sub"), "head", None), P(("groups", "dp", "sub"), "head"))
    return jax.shard_map(local, mesh=mesh, in_specs=in_specs, out_specs=out_specs, check_vma=False)
```

profile of v0, /device:TPU:80, one launch (start us, length us, event | category | flops | bytes accessed | tf_op | source)
XLA Modules:
  0.0 222.7 jit_solution(5330477741415702890)
XLA Ops:
  0.6 0.0 copy-start
  0.7 0.7 fusion.31
  1.4 0.1 gt.24
  1.5 0.1 gt.25
  1.6 0.7 bitcast_or_fusion
  2.3 0.1 reshape.484
  2.4 2.1 gather_fusion.1
  4.5 0.1 reshape.487
  4.6 0.1 select_n.160
  4.6 0.1 select_n.162
  4.7 0.1 gt.26
  4.8 0.1 select_n.158
  4.9 0.1 multiply_add_fusion
  5.0 0.9 reduce-window.6
  5.9 0.2 slice_reduce_fusion
  6.2 0.1 reshape.502
  6.2 0.1 fusion.25
  6.4 2.9 %scatter_custom_fusion.1 = s32[512]{0:T(512)S(1)} fusion(s32[384]{0:T(512)S(1)} %fusion.35, s32[384]{0:T(512)S(1)} %reshape.502, s32[]{:T(128)} %constant.86.clone.1), kind=kCustom, calls=%fused_computation.94 | custom fusion | bytes 2052 | tf_op jit(solution)/shard_map/scatter | solution.py:117
  9.3 0.1 reshape.465
  9.4 2.9 %scatter_custom_fusion = s32[512]{0:T(512)S(1)} fusion(s32[384]{0:T(512)S(1)} %fusion.35, s32[384]{0:T(512)S(1)} %get-tuple-element.17, s32[]{:T(128)} %constant.59.clone.1), kind=kCustom, calls=%fused_computation.97 | custom fusion | bytes 2052 | tf_op jit(solution)/shard_map/scatter | solution.py:113
  12.3 0.1 reshape.464
  12.4 0.7 pad_add_fusion
  13.1 44.4 %all-to-all-start = ((s32[32,1,32]{2,1,0:T(1,128)}), s32[32,1,32]{2,1,0:T(1,128)S(1)}, u32[]{:S(2)}, u32[]{:S(2)}) async-start(s32[32,1,32]{2,1,0:T(1,128)} %bitcast.3), calls=%async_computation | async-start | bytes 32768 | tf_op jit(solution)/shard_map/all_to_all | solution.py:17
  57.6 0.1 multiply_cosine_fusion
  57.7 0.1 subtract_convert_fusion
  57.8 0.1 pad_maximum_fusion
  57.9 11.4 %all-to-all-done = s32[32,1,32]{2,1,0:T(1,128)S(1)} async-done(((s32[32,1,32]{2,1,0:T(1,128)}), s32[32,1,32]{2,1,0:T(1,128)S(1)}, u32[]{:S(2)}, u32[]{:S(2)}) %all-to-all-start) | async-done | bytes 4128 | tf_op jit(solution)/shard_map/all_to_all | solution.py:17
  69.3 0.9 broadcast_in_dim.125
  70.2 4.8 %all-to-all-start.1 = ((bf16[32,8,1,8,128]{4,3,2,1,0:T(8,128)(2,1)}), bf16[32,8,1,8,128]{4,3,2,1,0:T(8,128)(2,1)S(1)}, u32[]{:S(2)}, u32[]{:S(2)}) async-start(bf16[32,8,1,8,128]{4,3,2,1,0:T(8,128)(2,1)} %broadcast_in_dim.125), calls=%async_computation.1 | async-start | bytes 1048576 | tf_op jit(solution)/shard_map/all_to_all | solution.py:32
  75.0 0.1 add_select_fusion
  75.1 0.1 broadcast_add_fusion
  75.2 0.1 reshape.468
  75.2 0.1 reshape.466
  75.3 0.1 eq.66
  75.4 4.8 %fusion.2 = bf16[64,8,32,128]{3,1,2,0:T(8,128)(2,1)S(1)} fusion(bf16[64,8,32,128]{3,2,1,0:T(8,128)(2,1)} %bitcast.82, s32[512]{0:T(512)S(1)} %eq.66), kind=kOutput, calls=%fused_computation.7 | convolution fusion | flops 2149842944 | bytes 8390656 | tf_op jit(solution)/shard_map/dot_general | solution.py:59
  80.2 3.2 %copy.97 = bf16[64,8,32,128]{3,2,1,0:T(8,128)(2,1)} copy(bf16[64,8,32,128]{3,1,2,0:T(8,128)(2,1)S(1)} %fusion.2) | data formatting | bytes 8388608
  83.4 0.1 lt.70
  83.5 0.1 copy.73
  83.5 0.1 copy.79
  83.7 0.1 iota_compare_fusion.2
  83.9 24.3 %all-to-all-done.1 = bf16[32,8,1,8,128]{4,3,2,1,0:T(8,128)(2,1)S(1)} async-done(((bf16[32,8,1,8,128]{4,3,2,1,0:T(8,128)(2,1)}), bf16[32,8,1,8,128]{4,3,2,1,0:T(8,128)(2,1)S(1)}, u32[]{:S(2)}, u32[]{:S(2)}) %all-to-all-start.1) | async-done | bytes 524320 | tf_op jit(solution)/shard_map/all_to_all | solution.py:32
  108.1 1.8 gather_fusion
  110.0 4.5 %select_reduce_fusion = (f32[512,8]{1,0:T(8,128)S(1)}, f32[512,8,16]{2,1,0:T(8,128)S(1)}) fusion(pred[512,16]{1,0:T(8,128)(4,1)S(1)} %iota_compare_fusion.2, bf16[512,1,2,16,128]{4,3,2,0,1:T(8,128)(2,1)} %bitcast.69, bf16[512,8,128]{2,1,0:T(8,128)(2,1)S(1)} %gather_fusion, pred[512]{0:T(512)(128)(4,1)S(1)} %compare_and_fusion), kind=kOutput, calls=%fused_computation.16 | convolution fusion | flops 17494016 | bytes 3432960 | tf_op jit(solution)/shard_map/skgd,sktd->skgt/dot_general | solution.py:66
  114.5 1.4 fusion.5
  115.9 1.6 convert_reduce_fusion
  117.6 0.2 copy.75
  117.7 0.1 select_reduce_fusion.1
  117.8 0.7 copy.76
  118.6 4.9 %all-to-all-start.2 = ((f32[32,8,1,8]{1,3,2,0:T(8,128)}), f32[32,8,1,8]{1,3,2,0:T(8,128)S(1)}, u32[]{:S(2)}, u32[]{:S(2)}) async-start(f32[32,8,1,8]{1,3,2,0:T(8,128)} %copy.76), calls=%async_computation.2 | async-start | bytes 262144 | tf_op jit(solution)/shard_map/all_to_all | solution.py:135
  123.5 0.2 copy.86
  123.7 0.2 multiply_reduce_fusion
  123.9 0.1 copy.81
  124.0 0.1 copy.80
  124.1 0.8 copy.87
  124.9 15.0 %all-to-all-done.2 = f32[32,8,1,8]{1,3,2,0:T(8,128)S(1)} async-done(((f32[32,8,1,8]{1,3,2,0:T(8,128)}), f32[32,8,1,8]{1,3,2,0:T(8,128)S(1)}, u32[]{:S(2)}, u32[]{:S(2)}) %all-to-all-start.2) | async-done | bytes 8224 | tf_op jit(solution)/shard_map/all_to_all | solution.py:135
  139.9 4.8 %all-to-all-start.4 = ((f32[32,8,1,8]{1,3,2,0:T(8,128)}), f32[32,8,1,8]{1,3,2,0:T(8,128)S(1)}, u32[]{:S(2)}, u32[]{:S(2)}) async-start(f32[32,8,1,8]{1,3,2,0:T(8,128)} %copy.87), calls=%async_computation.4 | async-start | bytes 262144 | tf_op jit(solution)/shard_map/all_to_all | solution.py:136
  144.7 3.3 %fusion.9 = f32[32,8,1,8,128]{4,1,3,2,0:T(8,128)} fusion(f32[32,16,8,128]{3,2,1,0:T(8,128)S(1)} %bitcast.71, f32[32,8,8]{1,2,0:T(8,128)S(1)} %copy.81, f32[32,16,8]{1,2,0:T(8,128)S(1)} %copy.80, pred[32,8,16]{2,1,0:T(8,128)(4,1)S(1)} %copy.79), kind=kOutput, calls=%fused_computation.17 | convolution fusion | flops 50397184 | bytes 3174400 | tf_op jit(solution)/shard_map/vmap(rmkg,mkgd->rkgd)/dot_general | solution.py:87
  148.0 13.1 %all-to-all-done.4 = f32[32,8,1,8]{1,3,2,0:T(8,128)S(1)} async-done(((f32[32,8,1,8]{1,3,2,0:T(8,128)}), f32[32,8,1,8]{1,3,2,0:T(8,128)S(1)}, u32[]{:S(2)}, u32[]{:S(2)}) %all-to-all-start.4) | async-done | bytes 8224 | tf_op jit(solution)/shard_map/all_to_all | solution.py:136
  161.1 4.8 %all-to-all-start.3 = ((f32[32,8,1,8,128]{4,1,3,2,0:T(8,128)}), f32[32,8,1,8,128]{4,1,3,2,0:T(8,128)S(1)}, u32[]{:S(2)}, u32[]{:S(2)}) async-start(f32[32,8,1,8,128]{4,1,3,2,0:T(8,128)} %fusion.9), calls=%async_computation.3 | async-start | bytes 2097152 | tf_op jit(solution)/shard_map/all_to_all | solution.py:137
  166.0 0.7 copy.90
  166.7 54.9 %all-to-all-done.3 = f32[32,8,1,8,128]{4,1,3,2,0:T(8,128)S(1)} async-done(((f32[32,8,1,8,128]{4,1,3,2,0:T(8,128)}), f32[32,8,1,8,128]{4,1,3,2,0:T(8,128)S(1)}, u32[]{:S(2)}, u32[]{:S(2)}) %all-to-all-start.3) | async-done | bytes 1048608 | tf_op jit(solution)/shard_map/all_to_all | solution.py:137
  221.6 0.3 bitcast_reduce_fusion
  222.0 0.1 divide_convert_fusion
  222.0 0.6 copy.89
  (30 shorter events, 0.3 us)
Async XLA Ops:
  0.6 1.7 copy-start
  2.4 2.2 copy-start.3
  2.4 2.5 %copy-start.4 = (s32[8]{0:T(128)S(1)}, s32[8]{0:T(128)}, u32[]{:S(2)}) copy-start(s32[8]{0:T(128)} %param.9) | copy-start | bytes 100
  2.4 55.2 %copy-start.2 = (bf16[8,8,128]{2,1,0:T(8,128)(2,1)S(1)}, bf16[8,8,128]{2,1,0:T(8,128)(2,1)}, u32[]{:S(2)}) copy-start(bf16[8,8,128]{2,1,0:T(8,128)(2,1)} %param.6) | copy-start | bytes 49156
  2.4 55.2 %copy-start.5 = (s32[8]{0:T(128)S(1)}, s32[8]{0:T(128)}, u32[]{:S(2)}) copy-start(s32[8]{0:T(128)} %param.11) | copy-start | bytes 100
  13.1 56.2 %all-to-all-start = ((s32[32,1,32]{2,1,0:T(1,128)}), s32[32,1,32]{2,1,0:T(1,128)S(1)}, u32[]{:S(2)}, u32[]{:S(2)}) async-start(s32[32,1,32]{2,1,0:T(1,128)} %bitcast.3), calls=%async_computation | async-start | bytes 32768 | tf_op jit(solution)/shard_map/all_to_all | solution.py:17
  70.2 38.0 %all-to-all-start.1 = ((bf16[32,8,1,8,128]{4,3,2,1,0:T(8,128)(2,1)}), bf16[32,8,1,8,128]{4,3,2,1,0:T(8,128)(2,1)S(1)}, u32[]{:S(2)}, u32[]{:S(2)}) async-start(bf16[32,8,1,8,128]{4,3,2,1,0:T(8,128)(2,1)} %broadcast_in_dim.125), calls=%async_computation.1 | async-start | bytes 1048576 | tf_op jit(solution)/shard_map/all_to_all | solution.py:32
  109.9 4.5 %copy-start.1 = (bf16[64,8,32,128]{3,2,1,0:T(8,128)(2,1)S(1)}, bf16[64,8,32,128]{3,2,1,0:T(8,128)(2,1)}, u32[]{:S(2)}) copy-start(bf16[64,8,32,128]{3,2,1,0:T(8,128)(2,1)} %copy.97) | copy-start | bytes 12582916
  118.6 21.3 %all-to-all-start.2 = ((f32[32,8,1,8]{1,3,2,0:T(8,128)}), f32[32,8,1,8]{1,3,2,0:T(8,128)S(1)}, u32[]{:S(2)}, u32[]{:S(2)}) async-start(f32[32,8,1,8]{1,3,2,0:T(8,128)} %copy.76), calls=%async_computation.2 | async-start | bytes 262144 | tf_op jit(solution)/shard_map/all_to_all | solution.py:135
  139.9 21.1 %all-to-all-start.4 = ((f32[32,8,1,8]{1,3,2,0:T(8,128)}), f32[32,8,1,8]{1,3,2,0:T(8,128)S(1)}, u32[]{:S(2)}, u32[]{:S(2)}) async-start(f32[32,8,1,8]{1,3,2,0:T(8,128)} %copy.87), calls=%async_computation.4 | async-start | bytes 262144 | tf_op jit(solution)/shard_map/all_to_all | solution.py:136
  161.1 60.6 %all-to-all-start.3 = ((f32[32,8,1,8,128]{4,1,3,2,0:T(8,128)}), f32[32,8,1,8,128]{4,1,3,2,0:T(8,128)S(1)}, u32[]{:S(2)}, u32[]{:S(2)}) async-start(f32[32,8,1,8,128]{4,1,3,2,0:T(8,128)} %fusion.9), calls=%async_computation.3 | async-start | bytes 2097152 | tf_op jit(solution)/shard_map/all_to_all | solution.py:137
where the time goes:
time: 224 us; the launch traced here: 223 us
  waiting for transfers between devices  119 us (53%)
  starting transfers between devices  63.8 us (28%)
  local copies, waits for them, and re-layouts  18.8 us (8%)
  matrix products  14 us (6%)
  other arithmetic  6.37 us (3%)
    all_to_all x1, waiting for transfers between devices, local(): lax.all_to_all(part_merged, ('dp', 'sub'), split_axis=0, concat_axis=0, t...  54.9 us
    all_to_all x1, starting transfers between devices, side_by_side(): lax.all_to_all(both, axis, split_axis=split_dim, concat_axis=concat_dim,...  44.4 us
    all_to_all x1, waiting for transfers between devices, from_everyone(): lax.all_to_all(jnp.broadcast_to(value[None], (size, *value.shape)), axis,...  24.3 us
    all_to_all x1, waiting for transfers between devices, local(): lax.all_to_all(part_top, ('dp', 'sub'), split_axis=0, concat_axis=0, tile...  15 us
    all_to_all x1, waiting for transfers between devices, local(): lax.all_to_all(part_norm, ('dp', 'sub'), split_axis=0, concat_axis=0, til...  13.1 us
    all_to_all x1, waiting for transfers between devices, side_by_side(): lax.all_to_all(both, axis, split_axis=split_dim, concat_axis=concat_dim,...  11.4 us
    all_to_all x1, starting transfers between devices, local(): lax.all_to_all(part_top, ('dp', 'sub'), split_axis=0, concat_axis=0, tile...  4.95 us
    all_to_all x1, starting transfers between devices, local(): lax.all_to_all(part_merged, ('dp', 'sub'), split_axis=0, concat_axis=0, t...  4.84 us
  transfers between devices with their start and end apart: 5, of which 5 were waited for; matrix products, arithmetic and copies ran while one was open for 7% of the time, Pallas kernels for 0%

commit v1 on v0

v1 whole, which is shorter than its diff:
```python
import jax
import jax.numpy as jnp
from jax import lax
from jax.experimental import pallas as pl
from jax.experimental.pallas import tpu as pltpu
from jax.sharding import PartitionSpec as P

LANES = 128
LOW = -1e30


def iota(shape, dim):
    return lax.broadcasted_iota(jnp.int32, shape, dim)


def bits(n):
    assert n & (n - 1) == 0
    return n.bit_length() - 1


def angles(positions, head_dim):
    half = head_dim // 2
    inverse = 1000000.0 ** (-(2.0 * jnp.arange(half, dtype=jnp.float32)) / head_dim)
    angle = positions.astype(jnp.float32)[:, None] * inverse[None, :]
    cosine, sine = jnp.cos(angle), jnp.sin(angle)
    return jnp.concatenate([cosine, cosine], axis=1), jnp.concatenate([-sine, sine], axis=1)


def pack(queries, cosine, sine, keep, lengths, placement, chips, cores, pool_dev, block_len):
    requests, heads, head_dim = queries.shape
    kept, blocks = keep.shape[1], placement.shape[1]
    owners = chips * cores
    spread = requests * blocks // owners
    rows = requests * heads
    parts = requests * blocks // LANES
    per = requests // parts
    assert per * blocks == LANES and 4 * cores * spread == LANES and head_dim == LANES
    pool_bits, owner_bits, len_bits, req_bits = bits(pool_dev), bits(cores), bits(block_len), bits(requests)

    def body(lengths_ref, q_ref, cos_ref, sin_ref, keep_ref, place_ref, out_ref):
        place = place_ref[...]
        kept_ids = keep_ref[...]
        req = iota((requests, blocks), 0)
        lane = iota((requests, blocks), 1)
        length = jnp.zeros((requests, blocks), jnp.int32)
        for r in range(requests):
            length = jnp.where(req == r, lengths_ref[r], length)
        count = jnp.zeros((requests, blocks), jnp.int32)
        for s in range(kept):
            count = jnp.where(kept_ids[:, s : s + 1] == lane, jnp.clip(length - s * block_len, 0, block_len), count)
        owner = place >> pool_bits
        owner = (owner & (cores - 1)) * chips + (owner >> owner_bits)
        word = (place & (pool_dev - 1)) | (req << pool_bits) | (count << (pool_bits + req_bits))
        owner = jnp.concatenate([owner[p * parts : (p + 1) * parts] for p in range(per)], axis=1)
        word = jnp.concatenate([word[p * parts : (p + 1) * parts] for p in range(per)], axis=1).astype(jnp.float32)
        mine = iota((owners, LANES), 0)
        hits = [owner[j : j + 1] == mine for j in range(parts)]
        ones = jnp.concatenate([jnp.where(h, 1.0, 0.0) for h in hits], axis=0).astype(jnp.bfloat16)
        before = jnp.where(iota((LANES, LANES), 0) < iota((LANES, LANES), 1), 1.0, 0.0).astype(jnp.bfloat16)
        within = jnp.dot(ones, before, preferred_element_type=jnp.float32)
        totals = jnp.dot(ones, jnp.ones((LANES, LANES), jnp.bfloat16), preferred_element_type=jnp.float32)
        ranks, start = [], jnp.zeros((owners, LANES), jnp.float32)
        for j in range(parts):
            ranks.append(jnp.where(hits[j], within[j * owners : (j + 1) * owners] + start, -1.0))
            start = start + totals[j * owners : (j + 1) * owners]
        col = iota((owners, LANES), 1)
        table = jnp.zeros((owners, LANES), jnp.float32)
        for k in range(spread):
            found = jnp.zeros((owners, LANES), jnp.float32)
            for j in range(parts):
                found = jnp.where(ranks[j] == k, word[j : j + 1], found)
            table = jnp.where((col & (spread - 1)) == k, jnp.sum(found, axis=1, keepdims=True), table)
        table = table.astype(jnp.int32)
        lane = iota((chips, LANES), 1)
        slots = table[:chips]
        for c in range(1, cores):
            slots = jnp.where(((lane >> bits(spread)) & (cores - 1)) == c, table[c * chips : (c + 1) * chips], slots)
        field = lane >> bits(spread * cores)
        low_bits = bits(block_len)
        row_hi = (slots & (pool_dev - 1)) >> low_bits
        row_lo = slots & (block_len - 1)
        of_req = (slots >> pool_bits) & (requests - 1)
        live = slots >> (pool_bits + req_bits)
        meta = jnp.where(field == 0, row_hi, jnp.where(field == 1, row_lo, jnp.where(field == 2, of_req, live)))
        meta = meta.astype(jnp.float32)
        turned = []
        for r in range(requests):
            x = q_ref[r].astype(jnp.float32)
            turned.append(x * cos_ref[r : r + 1] + pltpu.roll(x, head_dim // 2, 1) * sin_ref[r : r + 1])
        turned = jnp.concatenate(turned, axis=0).astype(jnp.bfloat16)
        sub = iota((8, LANES), 0)
        for d in range(chips):
            out_ref[d, :rows, :] = turned
            out_ref[d, rows:, :] = jnp.where(sub == 0, meta[d : d + 1], 0.0).astype(jnp.bfloat16)

    vmem = pl.BlockSpec(memory_space=pltpu.VMEM)
    return pl.pallas_call(
        body,
        name="pack",
        out_shape=jax.ShapeDtypeStruct((chips, rows + 8, LANES), jnp.bfloat16),
        in_specs=[pl.BlockSpec(memory_space=pltpu.SMEM)] + [vmem] * 5,
        out_specs=vmem,
    )(lengths, queries, cosine, sine, keep, placement)


def attend(core, kv, got, requests, block_len):
    cores, chips, height, _ = got.shape
    rows = height - 8
    heads = rows // requests
    sources = cores * chips
    spread = LANES // (4 * cores)
    tokens = spread * block_len
    factor = LANES ** (-0.5)
    height_out = chips * rows + rows

    def body(core_ref, kv_ref, got_ref, out_ref, ids_ref, live_ref, rows_ref, sem):
        at = core_ref[0] * spread
        meta = jnp.concatenate(
            [got_ref[c, z, rows:, :].astype(jnp.float32)[:1] for c in range(cores) for z in range(chips)], axis=0
        ).astype(jnp.bfloat16)
        wide = cores * spread
        src, dst = iota((LANES, LANES), 0), iota((LANES, LANES), 1)
        inside = dst < spread
        pick = jnp.where(inside & (src == at + dst), float(block_len), 0.0) + jnp.where(inside & (src == wide + at + dst), 1.0, 0.0)
        ids = jnp.dot(meta, pick.astype(jnp.bfloat16), preferred_element_type=jnp.float32)
        ids_ref[...] = ids.astype(jnp.int32)
        copy = pltpu.make_async_copy(ids_ref, rows_ref, sem)
        copy.start()
        src, dst = iota((LANES, tokens), 0), iota((LANES, tokens), 1) >> bits(block_len)
        pick_req = jnp.where(src == 2 * wide + at + dst, 1.0, 0.0).astype(jnp.bfloat16)
        pick_live = jnp.where(src == 3 * wide + at + dst, 1.0, 0.0).astype(jnp.bfloat16)
        of_req = jnp.dot(meta, pick_req, preferred_element_type=jnp.float32)
        count = jnp.dot(meta, pick_live, preferred_element_type=jnp.float32)
        step = (iota((sources, tokens), 1) & (block_len - 1)).astype(jnp.float32)
        live_ref[...] = jnp.where(step < count, of_req, -1.0)
        copy.wait()
        request = (iota((rows, tokens), 0) >> bits(heads)).astype(jnp.float32)
        lane = iota((rows, LANES), 1)
        fill = jnp.ones((tokens, LANES), jnp.bfloat16)

        for c in range(cores):

            def one(z, stats, c=c):
                s = c * chips + z
                q = got_ref[c, z, :rows, :]
                ks, vs = [], []
                for k in range(spread):
                    row = rows_ref[s, k]
                    ks.append(kv_ref[row, :block_len, :])
                    vs.append(kv_ref[row, block_len:, :])
                ks = jnp.concatenate(ks, axis=0)
                vs = jnp.concatenate([jnp.concatenate(vs, axis=0), fill], axis=1)
                score = lax.dot_general(q, ks, (((1,), (1,)), ((), ())), preferred_element_type=jnp.float32) * factor
                mine = live_ref[pl.ds(s, 1), :] == request
                score = jnp.where(mine, score, LOW)
                peak = jnp.max(score, axis=1, keepdims=True)
                weight = jnp.where(mine, jnp.exp(score - peak), 0.0).astype(jnp.bfloat16)
                both = jnp.dot(weight, vs, preferred_element_type=jnp.float32)
                total = both[:, LANES:]
                some = total > 0.0
                safe = jnp.where(some, total, 1.0)
                out_ref[c, pl.ds(pl.multiple_of(z * rows, rows), rows), :] = both[:, :LANES] / safe
                return jnp.where(lane == z, jnp.where(some, peak + jnp.log(safe), LOW), stats)

            stats = lax.fori_loop(0, chips, one, jnp.full((rows, LANES), LOW, jnp.float32), unroll=2)
            out_ref[c, chips * rows :, :] = stats

    vmem = pl.BlockSpec(memory_space=pltpu.VMEM)
    return pl.pallas_call(
        body,
        name="attend",
        out_shape=jax.ShapeDtypeStruct((cores, height_out, LANES), jnp.float32),
        in_specs=[pl.BlockSpec(memory_space=pltpu.SMEM), vmem, vmem],
        out_specs=vmem,
        scratch_shapes=[
            pltpu.VMEM((sources, LANES), jnp.int32),
            pltpu.VMEM((sources, tokens), jnp.float32),
            pltpu.SMEM((sources, LANES), jnp.int32),
            pltpu.SemaphoreType.DMA,
        ],
    )(core, kv, got)


def square(x):
    return jnp.concatenate([x, jnp.zeros((LANES - x.shape[0], LANES), x.dtype)], axis=0).T


def merge_pair(halves, chips):
    cores, height, _ = halves.shape
    rows = height // (chips + 1)

    def body(x_ref, out_ref):
        logs = [x_ref[c, chips * rows :, :] for c in range(cores)]
        top = logs[0]
        for one in logs[1:]:
            top = jnp.maximum(top, one)
        scale = [jnp.exp(one - top) for one in logs]
        norm = sum(scale[1:], scale[0])
        weight = [one / norm for one in scale]
        whole = square(top + jnp.log(norm))[:chips]
        first = whole.astype(jnp.bfloat16).astype(jnp.float32)
        rest = whole - first
        second = rest.astype(jnp.bfloat16).astype(jnp.float32)
        third = rest - second
        sub = iota((8, LANES), 0)
        for d in range(chips):
            mixed = sum(weight[c][:, d : d + 1] * x_ref[c, d * rows : (d + 1) * rows, :] for c in range(cores))
            out_ref[d, :rows, :] = mixed.astype(jnp.bfloat16)
            tail = jnp.where(sub == 0, first[d : d + 1], jnp.where(sub == 1, second[d : d + 1], third[d : d + 1]))
            out_ref[d, rows:, :] = tail.astype(jnp.bfloat16)

    vmem = pl.BlockSpec(memory_space=pltpu.VMEM)
    return pl.pallas_call(
        body,
        name="merge_pair",
        out_shape=jax.ShapeDtypeStruct((chips, rows + 8, LANES), jnp.bfloat16),
        in_specs=[vmem],
        out_specs=vmem,
    )(halves)


def finish(got, requests):
    chips, height, _ = got.shape
    rows = height - 8
    heads = rows // requests

    def body(x_ref, att_ref, log_ref):
        logs = []
        for s in range(chips):
            tail = x_ref[s, rows:, :].astype(jnp.float32)
            logs.append(tail[0:1] + tail[1:2] + tail[2:3])
        logs = jnp.concatenate(logs, axis=0)
        top = jnp.max(logs, axis=0, keepdims=True)
        scale = jnp.exp(logs - top)
        norm = jnp.sum(scale, axis=0, keepdims=True)
        log_norm = jnp.broadcast_to(top + jnp.log(norm), (requests, LANES))
        weight = square(scale / norm)[:rows]
        merged = sum(weight[:, s : s + 1] * x_ref[s, :rows, :].astype(jnp.float32) for s in range(chips))
        att_ref[...] = merged.reshape(requests, heads, LANES).astype(jnp.bfloat16)
        sub = iota((requests, LANES), 0)
        spread = log_norm
        for r in range(1, requests):
            spread = jnp.where(sub == r, pltpu.roll(log_norm, LANES - r * heads, 1), spread)
        log_ref[...] = spread[:, :heads]

    vmem = pl.BlockSpec(memory_space=pltpu.VMEM)
    return pl.pallas_call(
        body,
        name="finish",
        out_shape=(
            jax.ShapeDtypeStruct((requests, heads, LANES), jnp.bfloat16),
            jax.ShapeDtypeStruct((requests, heads), jnp.float32),
        ),
        in_specs=[vmem],
        out_specs=(vmem, vmem),
    )(got)


def local(queries, kv_cache, keep, lengths, placement, positions):
    chips, cores = lax.axis_size("dp"), lax.axis_size("sub")
    requests, q_heads, head_dim = queries.shape
    pool_dev, kv_heads, _, block_len, _ = kv_cache.shape
    assert kv_heads == 1
    cosine, sine = angles(positions, head_dim)
    message = pack(queries, cosine, sine, keep, lengths, placement, chips, cores, pool_dev, block_len)
    asked = lax.all_to_all(message, "dp", 0, 0, tiled=True)
    asked = lax.all_gather(asked, "sub")
    core = lax.axis_index("sub").reshape(1).astype(jnp.int32)
    partials = attend(core, kv_cache.reshape(pool_dev, 2 * block_len, head_dim), asked, requests, block_len)
    halves = lax.all_to_all(partials, "sub", 0, 0, tiled=True)
    answer = lax.all_to_all(merge_pair(halves, chips), "dp", 0, 0, tiled=True)
    return finish(answer, requests)


def solution(mesh):
    in_specs = (
        P(("groups", "dp", "sub"), "head", None),
        P(("groups", "dp", "sub"), "head", None, None, None),
        P(("groups", "dp", "sub"), None),
        P(("groups", "dp", "sub")),
        P(("groups", "dp", "sub"), None),
        P(("groups", "dp", "sub")),
    )
    out_specs = (P(("groups", "dp", "sub"), "head", None), P(("groups", "dp", "sub"), "head"))
    return jax.shard_map(local, mesh=mesh, in_specs=in_specs, out_specs=out_specs, check_vma=False)
```

time: 224 us -> 118 us (0.53)
  waiting for transfers between devices: 119 us -> 19.3 us
  blocking collectives: 0 us -> 35.2 us
  starting transfers between devices: 63.8 us -> 43.7 us
  local copies, waits for them, and re-layouts: 18.8 us -> 0 us
  Pallas kernels: 0 us -> 17.2 us
  matrix products: 14 us -> 0 us
  other arithmetic: 6.37 us -> 1.46 us
    all_to_all x5 -> x1, waiting for transfers between devices: 119 us -> 19.3 us  [local(): asked = lax.all_to_all(message, 'dp', 0, 0, tiled=True)]
    all_to_all x0 -> x2, blocking collectives: none -> 32.8 us  [the longest x1 26.1 us: local(): answer = lax.all_to_all(merge_pair(halves, chips), 'dp', 0, 0, tiled=True)]
    all_to_all x5 -> x1, starting transfers between devices: 63.8 us -> 43.7 us  [local(): asked = lax.all_to_all(message, 'dp', 0, 0, tiled=True)]
    pallas_call x0 -> x4, Pallas kernels: none -> 17.2 us  [the longest x1 10.9 us: attend(): pl.pallas_call(body, name='attend', out_shape=jax.ShapeDtypeStruct((cores...]
    dot_general x4 -> x0, matrix products: 14 us -> none  [the longest x1 4.77 us: select_rows(): jnp.dot(onehot, kv_cache.reshape(pool_dev, -1), preferred_element_type=jn...]
    scatter x2 -> x0, local copies, waits for them, and re-layouts: 5.82 us -> none  [the longest x1 2.91 us: local(): send_meta = jnp.zeros((owners * spread,), jnp.int32).at[target].set(reque...]
    unnamed x15 -> x0, local copies, waits for them, and re-layouts: 4.52 us -> none
    gather x4 -> x0, local copies, waits for them, and re-layouts: 4.01 us -> none  [the longest x3 2.21 us: local(): cache_rows = jnp.take_along_axis(placement, keep, axis=1)]
  transfers between devices with their start and end apart: 5 -> 1, of which waited for: 5 -> 1; matrix products, arithmetic and copies ran while one was open for 7% -> 0% of each run, Pallas kernels for 0% -> 0%
where the time goes in v1:
time: 118 us; the launch traced here: 117 us
  starting transfers between devices  43.7 us (37%)
  blocking collectives  35.2 us (30%)
  waiting for transfers between devices  19.3 us (16%)
  Pallas kernels  17.2 us (15%)
  other arithmetic  1.46 us (1%)
    all_to_all x1, starting transfers between devices, local(): asked = lax.all_to_all(message, 'dp', 0, 0, tiled=True)  43.7 us
    all_to_all x1, blocking collectives, local(): answer = lax.all_to_all(merge_pair(halves, chips), 'dp', 0, 0, tiled=True)  26.1 us
    all_to_all x1, waiting for transfers between devices, local(): asked = lax.all_to_all(message, 'dp', 0, 0, tiled=True)  19.3 us
    pallas_call x1, Pallas kernels, attend(): pl.pallas_call(body, name='attend', out_shape=jax.ShapeDtypeStruct((cores...  10.9 us
    all_to_all x1, blocking collectives, local(): halves = lax.all_to_all(partials, 'sub', 0, 0, tiled=True)  6.69 us
    all_gather x1, blocking collectives, local(): asked = lax.all_gather(asked, 'sub')  2.38 us
  transfers between devices with their start and end apart: 1, of which 1 were waited for; matrix products, arithmetic and copies ran while one was open for 0% of the time, Pallas kernels for 0%

profile of v1, /device:TPU:80, one launch (start us, length us, event | category | flops | bytes accessed | tf_op | source)
XLA Modules:
  0.0 117.5 jit_solution(6765959027195991161)
XLA Ops:
  0.6 0.7 convert_element_type.3
  1.3 0.1 fusion
  1.4 0.7 pad_maximum_fusion
  2.1 1.9 %pack.1 = bf16[16,72,128]{2,1,0:T(8,128)(2,1)} custom-call(s32[8]{0:T(128)} %lengths_ref.1, bf16[8,8,128]{2,1,0:T(8,128)(2,1)} %q_ref.1, f32[8,128]{1,0:T(8,128)} %get-tuple-element.5.cos_ref, f32[8,128]{1,0:T(8,128)} %get-tuple-element.6.sin_ref, s32[8,48]{1,0:T(8,128)} %keep_ref.1, s32[8,64]{1,0:T(8,128)} %place_ref.1), custom_call_target="tpu_custom_call" | custom-call | tf_op jit(solution)/shard_map/pack/pallas_call | solution.py:97
  4.0 43.7 %all-to-all-start = ((bf16[16,72,128]{2,1,0:T(8,128)(2,1)}), bf16[16,72,128]{2,1,0:T(8,128)(2,1)S(1)}, u32[]{:S(2)}, u32[]{:S(2)}) async-start(bf16[16,72,128]{2,1,0:T(8,128)(2,1)} %pack.1), calls=%async_computation | async-start | bytes 589824 | tf_op jit(solution)/shard_map/all_to_all | solution.py:266
  47.7 19.3 %all-to-all-done = bf16[16,72,128]{2,1,0:T(8,128)(2,1)S(1)} async-done(((bf16[16,72,128]{2,1,0:T(8,128)(2,1)}), bf16[16,72,128]{2,1,0:T(8,128)(2,1)S(1)}, u32[]{:S(2)}, u32[]{:S(2)}) %all-to-all-start) | async-done | bytes 294944 | tf_op jit(solution)/shard_map/all_to_all | solution.py:266
  67.0 2.4 %all-gather = bf16[32,72,128]{2,1,0:T(8,128)(2,1)} all-gather(bf16[16,72,128]{2,1,0:T(8,128)(2,1)S(1)} %all-to-all-done), channel_id=2, replica_groups=mesh['groups'=2,'dp'=16,'head'=8,'sub'=2] {'sub'}, dimensions={0}, use_global_device_ids=true | all-gather | bytes 884736 | tf_op jit(solution)/shard_map/all_gather | solution.py:267
  69.4 10.9 %attend.1 = f32[2,1088,128]{2,1,0:T(8,128)} custom-call(s32[1]{0:T(128)} %bitcast.core_ref, bf16[512,32,128]{2,1,0:T(8,128)(2,1)} %bitcast.3, bf16[2,16,72,128]{3,2,1,0:T(8,128)(2,1)} %bitcast.4), custom_call_target="tpu_custom_call" | custom-call | tf_op jit(solution)/shard_map/attend/pallas_call | solution.py:169
  80.4 6.7 %all_to_all.15.x_ref = f32[2,1088,128]{2,1,0:T(8,128)} all-to-all(f32[2,1088,128]{2,1,0:T(8,128)} %attend.1), channel_id=1, replica_groups=mesh['groups'=2,'dp'=16,'head'=8,'sub'=2] {'sub'}, dimensions={0} | all-to-all | bytes 2228224 | tf_op jit(solution)/shard_map/all_to_all | solution.py:270
  87.0 2.4 %merge_pair.1 = bf16[16,72,128]{2,1,0:T(8,128)(2,1)} custom-call(f32[2,1088,128]{2,1,0:T(8,128)} %all_to_all.15.x_ref), custom_call_target="tpu_custom_call" | custom-call | tf_op jit(solution)/shard_map/merge_pair/pallas_call | solution.py:213
  89.4 26.1 %all_to_all.16.x_ref = bf16[16,72,128]{2,1,0:T(8,128)(2,1)} all-to-all(bf16[16,72,128]{2,1,0:T(8,128)(2,1)} %merge_pair.1), channel_id=1, replica_groups=mesh['groups'=2,'dp'=16,'head'=8,'sub'=2] {'dp'}, dimensions={0} | all-to-all | bytes 589824 | tf_op jit(solution)/shard_map/all_to_all | solution.py:271
  115.5 2.0 %finish.1 = (bf16[8,8,128]{2,1,0:T(8,128)(2,1)}, f32[8,8]{1,0:T(8,128)}) custom-call(bf16[16,72,128]{2,1,0:T(8,128)(2,1)} %all_to_all.16.x_ref), custom_call_target="tpu_custom_call" | custom-call | tf_op jit(solution)/shard_map/finish/pallas_call | solution.py:247
  (1 shorter events, 0.0 us)
Async XLA Ops:
  4.0 63.0 %all-to-all-start = ((bf16[16,72,128]{2,1,0:T(8,128)(2,1)}), bf16[16,72,128]{2,1,0:T(8,128)(2,1)S(1)}, u32[]{:S(2)}, u32[]{:S(2)}) async-start(bf16[16,72,128]{2,1,0:T(8,128)(2,1)} %pack.1), calls=%async_computation | async-start | bytes 589824 | tf_op jit(solution)/shard_map/all_to_all | solution.py:266

commit v2 on v1

--- a/solution.py
+++ b/solution.py
@@ -1,5 +1,6 @@
 import jax
 import jax.numpy as jnp
+import numpy as np
 from jax import lax
 from jax.experimental import pallas as pl
 from jax.experimental.pallas import tpu as pltpu
@@ -7,6 +8,9 @@
 
 LANES = 128
 LOW = -1e30
+UNROLL = 4
+PACK_LIMIT = 60 * 1024
+ATTEND_LIMIT = 52000
 
 
 def iota(shape, dim):
@@ -18,15 +22,17 @@
     return n.bit_length() - 1
 
 
-def angles(positions, head_dim):
+def frequencies(head_dim, rows):
     half = head_dim // 2
-    inverse = 1000000.0 ** (-(2.0 * jnp.arange(half, dtype=jnp.float32)) / head_dim)
-    angle = positions.astype(jnp.float32)[:, None] * inverse[None, :]
-    cosine, sine = jnp.cos(angle), jnp.sin(angle)
-    return jnp.concatenate([cosine, cosine], axis=1), jnp.concatenate([-sine, sine], axis=1)
-
-
-def pack(queries, cosine, sine, keep, lengths, placement, chips, cores, pool_dev, block_len):
+    inverse = 1000000.0 ** (-(2.0 * np.arange(half)) / head_dim)
+    return jnp.asarray(np.tile(inverse, (rows, head_dim // half)), jnp.float32)
+
+
+def limit(kib):
+    return pltpu.CompilerParams(vmem_limit_bytes=kib << 10)
+
+
+def pack(queries, positions, keep, lengths, placement, chips, cores, pool_dev, block_len):
     requests, heads, head_dim = queries.shape
     kept, blocks = keep.shape[1], placement.shape[1]
     owners = chips * cores
@@ -37,7 +43,7 @@
     assert per * blocks == LANES and 4 * cores * spread == LANES and head_dim == LANES
     pool_bits, owner_bits, len_bits, req_bits = bits(pool_dev), bits(cores), bits(block_len), bits(requests)
 
-    def body(lengths_ref, q_ref, cos_ref, sin_ref, keep_ref, place_ref, out_ref):
+    def body(lengths_ref, positions_ref, q_ref, freq_ref, keep_ref, place_ref, out_ref):
         place = place_ref[...]
         kept_ids = keep_ref[...]
         req = iota((requests, blocks), 0)
@@ -83,10 +89,17 @@
         live = slots >> (pool_bits + req_bits)
         meta = jnp.where(field == 0, row_hi, jnp.where(field == 1, row_lo, jnp.where(field == 2, of_req, live)))
         meta = meta.astype(jnp.float32)
+        row = iota((requests, head_dim), 0)
+        position = jnp.zeros((requests, head_dim), jnp.int32)
+        for r in range(requests):
+            position = jnp.where(row == r, positions_ref[r], position)
+        angle = position.astype(jnp.float32) * freq_ref[...]
+        cosine, sine = jnp.cos(angle), jnp.sin(angle)
+        sine = jnp.where(iota((requests, head_dim), 1) < head_dim // 2, -sine, sine)
         turned = []
         for r in range(requests):
             x = q_ref[r].astype(jnp.float32)
-            turned.append(x * cos_ref[r : r + 1] + pltpu.roll(x, head_dim // 2, 1) * sin_ref[r : r + 1])
+            turned.append(x * cosine[r : r + 1] + pltpu.roll(x, head_dim // 2, 1) * sine[r : r + 1])
         turned = jnp.concatenate(turned, axis=0).astype(jnp.bfloat16)
         sub = iota((8, LANES), 0)
         for d in range(chips):
@@ -98,23 +111,35 @@
         body,
         name="pack",
         out_shape=jax.ShapeDtypeStruct((chips, rows + 8, LANES), jnp.bfloat16),
-        in_specs=[pl.BlockSpec(memory_space=pltpu.SMEM)] + [vmem] * 5,
+        in_specs=[pl.BlockSpec(memory_space=pltpu.SMEM)] * 2 + [vmem] * 4,
         out_specs=vmem,
-    )(lengths, queries, cosine, sine, keep, placement)
-
-
-def attend(core, kv, got, requests, block_len):
+        compiler_params=limit(PACK_LIMIT),
+    )(lengths, positions, queries, frequencies(head_dim, requests), keep, placement)
+
+
+def pieces(x):
+    first = x.astype(jnp.bfloat16).astype(jnp.float32)
+    rest = x - first
+    second = rest.astype(jnp.bfloat16).astype(jnp.float32)
+    return first, second, rest - second
+
+
+def attend(kv, got, requests):
     cores, chips, height, _ = got.shape
+    pool_dev, _, block_len, _ = kv.shape
     rows = height - 8
     heads = rows // requests
     sources = cores * chips
     spread = LANES // (4 * cores)
     tokens = spread * block_len
     factor = LANES ** (-0.5)
-    height_out = chips * rows + rows
-
-    def body(core_ref, kv_ref, got_ref, out_ref, ids_ref, live_ref, rows_ref, sem):
-        at = core_ref[0] * spread
+
+    def body(kv_ref, got_ref, out_ref, k_ref, v_ref, ids_ref, live_ref, weight_ref, rows_ref, sems):
+        k_copy = pltpu.make_async_copy(kv_ref.at[:, 0], k_ref, sems.at[0])
+        v_copy = pltpu.make_async_copy(kv_ref.at[:, 1], v_ref, sems.at[1])
+        k_copy.start()
+        v_copy.start()
+        at = lax.axis_index("sub") * spread
         meta = jnp.concatenate(
             [got_ref[c, z, rows:, :].astype(jnp.float32)[:1] for c in range(cores) for z in range(chips)], axis=0
         ).astype(jnp.bfloat16)
@@ -124,7 +149,7 @@
         pick = jnp.where(inside & (src == at + dst), float(block_len), 0.0) + jnp.where(inside & (src == wide + at + dst), 1.0, 0.0)
         ids = jnp.dot(meta, pick.astype(jnp.bfloat16), preferred_element_type=jnp.float32)
         ids_ref[...] = ids.astype(jnp.int32)
-        copy = pltpu.make_async_copy(ids_ref, rows_ref, sem)
+        copy = pltpu.make_async_copy(ids_ref, rows_ref, sems.at[2])
         copy.start()
         src, dst = iota((LANES, tokens), 0), iota((LANES, tokens), 1) >> bits(block_len)
         pick_req = jnp.where(src == 2 * wide + at + dst, 1.0, 0.0).astype(jnp.bfloat16)
@@ -133,52 +158,72 @@
         count = jnp.dot(meta, pick_live, preferred_element_type=jnp.float32)
         step = (iota((sources, tokens), 1) & (block_len - 1)).astype(jnp.float32)
         live_ref[...] = jnp.where(step < count, of_req, -1.0)
-        copy.wait()
         request = (iota((rows, tokens), 0) >> bits(heads)).astype(jnp.float32)
         lane = iota((rows, LANES), 1)
         fill = jnp.ones((tokens, LANES), jnp.bfloat16)
-
+        low = jnp.full((rows, LANES), LOW, jnp.float32)
+        copy.wait()
+        k_copy.wait()
+
+        def held(ref, s):
+            return jnp.concatenate([ref[rows_ref[s, k]] for k in range(spread)], axis=0)
+
+        peaks = []
         for c in range(cores):
 
-            def one(z, stats, c=c):
+            def look(z, peak_of, c=c):
                 s = c * chips + z
-                q = got_ref[c, z, :rows, :]
-                ks, vs = [], []
-                for k in range(spread):
-                    row = rows_ref[s, k]
-                    ks.append(kv_ref[row, :block_len, :])
-                    vs.append(kv_ref[row, block_len:, :])
-                ks = jnp.concatenate(ks, axis=0)
-                vs = jnp.concatenate([jnp.concatenate(vs, axis=0), fill], axis=1)
-                score = lax.dot_general(q, ks, (((1,), (1,)), ((), ())), preferred_element_type=jnp.float32) * factor
+                score = (
+                    lax.dot_general(
+                        got_ref[c, z, :rows, :], held(k_ref, s), (((1,), (1,)), ((), ())), preferred_element_type=jnp.float32
+                    )
+                    * factor
+                )
                 mine = live_ref[pl.ds(s, 1), :] == request
                 score = jnp.where(mine, score, LOW)
                 peak = jnp.max(score, axis=1, keepdims=True)
-                weight = jnp.where(mine, jnp.exp(score - peak), 0.0).astype(jnp.bfloat16)
-                both = jnp.dot(weight, vs, preferred_element_type=jnp.float32)
+                weight_ref[s] = jnp.where(mine, jnp.exp(score - peak), 0.0).astype(jnp.bfloat16)
+                return jnp.where(lane == z, peak, peak_of)
+
+            peaks.append(lax.fori_loop(0, chips, look, low, unroll=UNROLL))
+        v_copy.wait()
+        for c in range(cores):
+
+            def add(z, total_of, c=c):
+                s = c * chips + z
+                vs = jnp.concatenate([held(v_ref, s), fill], axis=1)
+                both = jnp.dot(weight_ref[s], vs, preferred_element_type=jnp.float32)
                 total = both[:, LANES:]
-                some = total > 0.0
-                safe = jnp.where(some, total, 1.0)
-                out_ref[c, pl.ds(pl.multiple_of(z * rows, rows), rows), :] = both[:, :LANES] / safe
-                return jnp.where(lane == z, jnp.where(some, peak + jnp.log(safe), LOW), stats)
-
-            stats = lax.fori_loop(0, chips, one, jnp.full((rows, LANES), LOW, jnp.float32), unroll=2)
-            out_ref[c, chips * rows :, :] = stats
+                safe = jnp.where(total > 0.0, total, 1.0)
+                out_ref[c, pl.ds(pl.multiple_of(z * rows, rows), rows), :] = (both[:, :LANES] / safe).astype(jnp.bfloat16)
+                return jnp.where(lane == z, total, total_of)
+
+            total = lax.fori_loop(0, chips, add, jnp.zeros((rows, LANES), jnp.float32), unroll=UNROLL)
+            some = total > 0.0
+            first, second, third = pieces(jnp.where(some, peaks[c] + jnp.log(jnp.where(some, total, 1.0)), LOW))
+            second, third = pltpu.roll(second, chips, 1), pltpu.roll(third, 2 * chips, 1)
+            out_ref[c, chips * rows :, :] = jnp.where(
+                lane < chips, first, jnp.where(lane < 2 * chips, second, third)
+            ).astype(jnp.bfloat16)
 
     vmem = pl.BlockSpec(memory_space=pltpu.VMEM)
     return pl.pallas_call(
         body,
         name="attend",
-        out_shape=jax.ShapeDtypeStruct((cores, height_out, LANES), jnp.float32),
-        in_specs=[pl.BlockSpec(memory_space=pltpu.SMEM), vmem, vmem],
+        out_shape=jax.ShapeDtypeStruct((cores, chips * rows + rows, LANES), jnp.bfloat16),
+        in_specs=[pl.BlockSpec(memory_space=pltpu.HBM), vmem],
         out_specs=vmem,
+        compiler_params=limit(ATTEND_LIMIT),
         scratch_shapes=[
+            pltpu.VMEM((pool_dev, block_len, LANES), jnp.bfloat16),
+            pltpu.VMEM((pool_dev, block_len, LANES), jnp.bfloat16),
             pltpu.VMEM((sources, LANES), jnp.int32),
             pltpu.VMEM((sources, tokens), jnp.float32),
+            pltpu.VMEM((sources, rows, tokens), jnp.bfloat16),
             pltpu.SMEM((sources, LANES), jnp.int32),
-            pltpu.SemaphoreType.DMA,
+            pltpu.SemaphoreType.DMA((3,)),
         ],
-    )(core, kv, got)
+    )(kv, got)
 
 
 def square(x):
@@ -190,7 +235,10 @@
     rows = height // (chips + 1)
 
     def body(x_ref, out_ref):
-        logs = [x_ref[c, chips * rows :, :] for c in range(cores)]
+        logs = []
+        for c in range(cores):
+            tail = x_ref[c, chips * rows :, :].astype(jnp.float32)
+            logs.append(tail + pltpu.roll(tail, LANES - chips, 1) + pltpu.roll(tail, LANES - 2 * chips, 1))
         top = logs[0]
         for one in logs[1:]:
             top = jnp.maximum(top, one)
@@ -198,13 +246,12 @@
         norm = sum(scale[1:], scale[0])
         weight = [one / norm for one in scale]
         whole = square(top + jnp.log(norm))[:chips]
-        first = whole.astype(jnp.bfloat16).astype(jnp.float32)
-        rest = whole - first
-        second = rest.astype(jnp.bfloat16).astype(jnp.float32)
-        third = rest - second
+        first, second, third = pieces(whole)
         sub = iota((8, LANES), 0)
         for d in range(chips):
-            mixed = sum(weight[c][:, d : d + 1] * x_ref[c, d * rows : (d + 1) * rows, :] for c in range(cores))
+            mixed = sum(
+                weight[c][:, d : d + 1] * x_ref[c, d * rows : (d + 1) * rows, :].astype(jnp.float32) for c in range(cores)
+            )
             out_ref[d, :rows, :] = mixed.astype(jnp.bfloat16)
             tail = jnp.where(sub == 0, first[d : d + 1], jnp.where(sub == 1, second[d : d + 1], third[d : d + 1]))
             out_ref[d, rows:, :] = tail.astype(jnp.bfloat16)
@@ -216,6 +263,7 @@
         out_shape=jax.ShapeDtypeStruct((chips, rows + 8, LANES), jnp.bfloat16),
         in_specs=[vmem],
         out_specs=vmem,
+        compiler_params=limit(4096),
     )(halves)
 
 
@@ -253,6 +301,7 @@
         ),
         in_specs=[vmem],
         out_specs=(vmem, vmem),
+        compiler_params=limit(4096),
     )(got)
 
 
@@ -261,12 +310,10 @@
     requests, q_heads, head_dim = queries.shape
     pool_dev, kv_heads, _, block_len, _ = kv_cache.shape
     assert kv_heads == 1
-    cosine, sine = angles(positions, head_dim)
-    message = pack(queries, cosine, sine, keep, lengths, placement, chips, cores, pool_dev, block_len)
+    message = pack(queries, positions, keep, lengths, placement, chips, cores, pool_dev, block_len)
     asked = lax.all_to_all(message, "dp", 0, 0, tiled=True)
     asked = lax.all_gather(asked, "sub")
-    core = lax.axis_index("sub").reshape(1).astype(jnp.int32)
-    partials = attend(core, kv_cache.reshape(pool_dev, 2 * block_len, head_dim), asked, requests, block_len)
+    partials = attend(kv_cache.reshape(pool_dev, 2, block_len, head_dim), asked, requests)
     halves = lax.all_to_all(partials, "sub", 0, 0, tiled=True)
     answer = lax.all_to_all(merge_pair(halves, chips), "dp", 0, 0, tiled=True)
     return finish(answer, requests)

time: 118 us -> 106 us (0.90)
  blocking collectives: 35.2 us -> 95.2 us
  starting transfers between devices: 43.7 us -> 0 us
  waiting for transfers between devices: 19.3 us -> 0 us
  Pallas kernels: 17.2 us -> 9.45 us
  other arithmetic: 1.46 us -> 0 us
    all_to_all x0 -> x1, blocking collectives: none -> 63 us  [local(): asked = lax.all_to_all(message, 'dp', 0, 0, tiled=True)]
    all_to_all x1 -> x0, starting transfers between devices: 43.7 us -> none  [local(): asked = lax.all_to_all(message, 'dp', 0, 0, tiled=True)]
    all_to_all x1 -> x0, waiting for transfers between devices: 19.3 us -> none  [local(): asked = lax.all_to_all(message, 'dp', 0, 0, tiled=True)]
    pallas_call x1, Pallas kernels: 10.9 us -> 6.04 us  [attend(): pl.pallas_call(body, name='attend', out_shape=jax.ShapeDtypeStruct((cores...]
    all_to_all x1, blocking collectives: 6.69 us -> 4.18 us  [local(): halves = lax.all_to_all(partials, 'sub', 0, 0, tiled=True)]
    pallas_call x1, Pallas kernels: 2.35 us -> 0.49 us  [merge_pair(): pl.pallas_call(body, name='merge_pair', out_shape=jax.ShapeDtypeStruct((c...]
  transfers between devices with their start and end apart: 1 -> 0, of which waited for: 1 -> 0; matrix products, arithmetic and copies ran while one was open for 0% -> 0% of each run, Pallas kernels for 0% -> 0%
where the time goes in v2:
time: 106 us; the launch traced here: 105 us
  blocking collectives  95.2 us (90%)
  Pallas kernels  9.45 us (9%)
    all_to_all x1, blocking collectives, local(): asked = lax.all_to_all(message, 'dp', 0, 0, tiled=True)  63 us
    all_to_all x1, blocking collectives, local(): answer = lax.all_to_all(merge_pair(halves, chips), 'dp', 0, 0, tiled=True)  25.8 us
    pallas_call x1, Pallas kernels, attend(): pl.pallas_call(body, name='attend', out_shape=jax.ShapeDtypeStruct((cores...  6.04 us
    all_to_all x1, blocking collectives, local(): halves = lax.all_to_all(partials, 'sub', 0, 0, tiled=True)  4.18 us
    all_gather x1, blocking collectives, local(): asked = lax.all_gather(asked, 'sub')  2.25 us

profile of v2, /device:TPU:80, one launch (start us, length us, event | category | flops | bytes accessed | tf_op | source)
XLA Modules:
  0.0 105.3 jit_solution(11676295918039457237)
XLA Ops:
  0.6 1.9 %pack.1 = bf16[16,72,128]{2,1,0:T(8,128)(2,1)} custom-call(s32[8]{0:T(128)} %lengths_ref.1, s32[8]{0:T(128)} %positions_ref.1, bf16[8,8,128]{2,1,0:T(8,128)(2,1)} %q_ref.1, f32[8,128]{1,0:T(8,128)} %constant.2.clone.freq_ref, s32[8,48]{1,0:T(8,128)} %keep_ref.1, s32[8,64]{1,0:T(8,128)} %place_ref.1), custom_call_target="tpu_custom_call" | custom-call | tf_op jit(solution)/shard_map/pack/pallas_call | solution.py:110
  2.6 63.0 %all_to_all.15 = bf16[16,72,128]{2,1,0:T(8,128)(2,1)S(1)} all-to-all(bf16[16,72,128]{2,1,0:T(8,128)(2,1)} %pack.1), channel_id=1, replica_groups=mesh['groups'=2,'dp'=16,'head'=8,'sub'=2] {'dp'}, dimensions={0} | all-to-all | bytes 589824 | tf_op jit(solution)/shard_map/all_to_all | solution.py:314
  65.6 2.2 %all-gather = bf16[32,72,128]{2,1,0:T(8,128)(2,1)S(1)} all-gather(bf16[16,72,128]{2,1,0:T(8,128)(2,1)S(1)} %all_to_all.15), channel_id=2, replica_groups=mesh['groups'=2,'dp'=16,'head'=8,'sub'=2] {'sub'}, dimensions={0}, use_global_device_ids=true | all-gather | bytes 884736 | tf_op jit(solution)/shard_map/all_gather | solution.py:315
  67.8 6.0 %attend.1 = bf16[2,1088,128]{2,1,0:T(8,128)(2,1)S(1)} custom-call(bf16[512,2,16,128]{3,2,1,0:T(8,128)(2,1)} %bitcast.3, bf16[2,16,72,128]{3,2,1,0:T(8,128)(2,1)S(1)} %bitcast.2), custom_call_target="tpu_custom_call" | custom-call | tf_op jit(solution)/shard_map/attend/pallas_call | solution.py:210
  73.9 4.2 %all_to_all.16.x_ref = bf16[2,1088,128]{2,1,0:T(8,128)(2,1)S(1)} all-to-all(bf16[2,1088,128]{2,1,0:T(8,128)(2,1)S(1)} %attend.1), channel_id=1, replica_groups=mesh['groups'=2,'dp'=16,'head'=8,'sub'=2] {'sub'}, dimensions={0} | all-to-all | bytes 1114112 | tf_op jit(solution)/shard_map/all_to_all | solution.py:317
  78.0 0.5 merge_pair.1
  78.5 25.8 %all_to_all.17.x_ref = bf16[16,72,128]{2,1,0:T(8,128)(2,1)S(1)} all-to-all(bf16[16,72,128]{2,1,0:T(8,128)(2,1)S(1)} %merge_pair.1), channel_id=1, replica_groups=mesh['groups'=2,'dp'=16,'head'=8,'sub'=2] {'dp'}, dimensions={0} | all-to-all | bytes 589824 | tf_op jit(solution)/shard_map/all_to_all | solution.py:318
  104.3 1.0 finish.1

commit v3 on v2

--- a/solution.py
+++ b/solution.py
@@ -8,7 +8,9 @@
 
 LANES = 128
 LOW = -1e30
-UNROLL = 4
+LOG2E = 1.4426950408889634
+NEAR = 2
+UNROLL = True
 PACK_LIMIT = 60 * 1024
 ATTEND_LIMIT = 52000
 
@@ -32,7 +34,7 @@
     return pltpu.CompilerParams(vmem_limit_bytes=kib << 10)
 
 
-def pack(queries, positions, keep, lengths, placement, chips, cores, pool_dev, block_len):
+def pack(queries, positions, keep, lengths, placement, chips, near, cores, pool_dev, block_len):
     requests, heads, head_dim = queries.shape
     kept, blocks = keep.shape[1], placement.shape[1]
     owners = chips * cores
@@ -102,15 +104,18 @@
             turned.append(x * cosine[r : r + 1] + pltpu.roll(x, head_dim // 2, 1) * sine[r : r + 1])
         turned = jnp.concatenate(turned, axis=0).astype(jnp.bfloat16)
         sub = iota((8, LANES), 0)
-        for d in range(chips):
+        for d in range(chips // near):
             out_ref[d, :rows, :] = turned
-            out_ref[d, rows:, :] = jnp.where(sub == 0, meta[d : d + 1], 0.0).astype(jnp.bfloat16)
+            tail = jnp.zeros((8, LANES), jnp.float32)
+            for p in range(near):
+                tail = jnp.where(sub == p, meta[d * near + p : d * near + p + 1], tail)
+            out_ref[d, rows:, :] = tail.astype(jnp.bfloat16)
 
     vmem = pl.BlockSpec(memory_space=pltpu.VMEM)
     return pl.pallas_call(
         body,
         name="pack",
-        out_shape=jax.ShapeDtypeStruct((chips, rows + 8, LANES), jnp.bfloat16),
+        out_shape=jax.ShapeDtypeStruct((chips // near, rows + 8, LANES), jnp.bfloat16),
         in_specs=[pl.BlockSpec(memory_space=pltpu.SMEM)] * 2 + [vmem] * 4,
         out_specs=vmem,
         compiler_params=limit(PACK_LIMIT),
@@ -125,24 +130,27 @@
 
 
 def attend(kv, got, requests):
-    cores, chips, height, _ = got.shape
+    cores, near, far, height, _ = got.shape
     pool_dev, _, block_len, _ = kv.shape
+    chips = near * far
     rows = height - 8
     heads = rows // requests
     sources = cores * chips
     spread = LANES // (4 * cores)
     tokens = spread * block_len
-    factor = LANES ** (-0.5)
-
-    def body(kv_ref, got_ref, out_ref, k_ref, v_ref, ids_ref, live_ref, weight_ref, rows_ref, sems):
+    factor = LANES ** (-0.5) * LOG2E
+    assert cores == 2
+
+    def body(kv_ref, got_ref, send_ref, keep_ref, k_ref, v_ref, ids_ref, live_ref, weight_ref, rows_ref, sems):
         k_copy = pltpu.make_async_copy(kv_ref.at[:, 0], k_ref, sems.at[0])
         v_copy = pltpu.make_async_copy(kv_ref.at[:, 1], v_ref, sems.at[1])
         k_copy.start()
-        v_copy.start()
-        at = lax.axis_index("sub") * spread
-        meta = jnp.concatenate(
-            [got_ref[c, z, rows:, :].astype(jnp.float32)[:1] for c in range(cores) for z in range(chips)], axis=0
-        ).astype(jnp.bfloat16)
+        me = lax.axis_index("sub")
+        at = me * spread
+        tails = jnp.concatenate([got_ref[s // chips, s % chips, rows:, :] for s in range(sources)], axis=0)
+        mine_row = iota((sources, 8 * sources), 0) * 8 + lax.axis_index("dp") % near
+        select = jnp.where(iota((sources, 8 * sources), 1) == mine_row, 1.0, 0.0).astype(jnp.bfloat16)
+        meta = jnp.dot(select, tails, preferred_element_type=jnp.float32).astype(jnp.bfloat16)
         wide = cores * spread
         src, dst = iota((LANES, LANES), 0), iota((LANES, LANES), 1)
         inside = dst < spread
@@ -163,56 +171,64 @@
         fill = jnp.ones((tokens, LANES), jnp.bfloat16)
         low = jnp.full((rows, LANES), LOW, jnp.float32)
         copy.wait()
+        v_copy.start()
         k_copy.wait()
 
         def held(ref, s):
             return jnp.concatenate([ref[rows_ref[s, k]] for k in range(spread)], axis=0)
 
+        def chip(i):
+            return (i & (far - 1)) * near + (i >> bits(far))
+
+        whose = (1 - me, me)
         peaks = []
-        for c in range(cores):
-
-            def look(z, peak_of, c=c):
-                s = c * chips + z
+        for c in whose:
+
+            def look(i, peak_of, c=c):
+                s = c * chips + i
                 score = (
                     lax.dot_general(
-                        got_ref[c, z, :rows, :], held(k_ref, s), (((1,), (1,)), ((), ())), preferred_element_type=jnp.float32
+                        got_ref[c, i, :rows, :], held(k_ref, s), (((1,), (1,)), ((), ())), preferred_element_type=jnp.float32
                     )
                     * factor
                 )
                 mine = live_ref[pl.ds(s, 1), :] == request
                 score = jnp.where(mine, score, LOW)
                 peak = jnp.max(score, axis=1, keepdims=True)
-                weight_ref[s] = jnp.where(mine, jnp.exp(score - peak), 0.0).astype(jnp.bfloat16)
-                return jnp.where(lane == z, peak, peak_of)
+                weight_ref[s] = jnp.where(mine, jnp.exp2(score - peak), 0.0).astype(jnp.bfloat16)
+                return jnp.where(lane == chip(i), peak, peak_of)
 
             peaks.append(lax.fori_loop(0, chips, look, low, unroll=UNROLL))
         v_copy.wait()
-        for c in range(cores):
-
-            def add(z, total_of, c=c):
-                s = c * chips + z
+        for c, peak_of, out_ref in zip(whose, peaks, (send_ref, keep_ref)):
+
+            def add(i, total_of, c=c, out_ref=out_ref):
+                s = c * chips + i
                 vs = jnp.concatenate([held(v_ref, s), fill], axis=1)
                 both = jnp.dot(weight_ref[s], vs, preferred_element_type=jnp.float32)
                 total = both[:, LANES:]
                 safe = jnp.where(total > 0.0, total, 1.0)
-                out_ref[c, pl.ds(pl.multiple_of(z * rows, rows), rows), :] = (both[:, :LANES] / safe).astype(jnp.bfloat16)
-                return jnp.where(lane == z, total, total_of)
+                start = pl.multiple_of(chip(i) * rows, rows)
+                out_ref[pl.ds(start, rows), :] = (both[:, :LANES] / safe).astype(jnp.bfloat16)
+                return jnp.where(lane == chip(i), total, total_of)
 
             total = lax.fori_loop(0, chips, add, jnp.zeros((rows, LANES), jnp.float32), unroll=UNROLL)
             some = total > 0.0
-            first, second, third = pieces(jnp.where(some, peaks[c] + jnp.log(jnp.where(some, total, 1.0)), LOW))
+            logs = peak_of * (1.0 / LOG2E) + jnp.log(jnp.where(some, total, 1.0))
+            first, second, third = pieces(jnp.where(some, logs, LOW))
             second, third = pltpu.roll(second, chips, 1), pltpu.roll(third, 2 * chips, 1)
-            out_ref[c, chips * rows :, :] = jnp.where(
+            out_ref[chips * rows :, :] = jnp.where(
                 lane < chips, first, jnp.where(lane < 2 * chips, second, third)
             ).astype(jnp.bfloat16)
 
     vmem = pl.BlockSpec(memory_space=pltpu.VMEM)
+    half = jax.ShapeDtypeStruct((chips * rows + rows, LANES), jnp.bfloat16)
     return pl.pallas_call(
         body,
         name="attend",
-        out_shape=jax.ShapeDtypeStruct((cores, chips * rows + rows, LANES), jnp.bfloat16),
+        out_shape=(half, half),
         in_specs=[pl.BlockSpec(memory_space=pltpu.HBM), vmem],
-        out_specs=vmem,
+        out_specs=(vmem, vmem),
         compiler_params=limit(ATTEND_LIMIT),
         scratch_shapes=[
             pltpu.VMEM((pool_dev, block_len, LANES), jnp.bfloat16),
@@ -223,7 +239,7 @@
             pltpu.SMEM((sources, LANES), jnp.int32),
             pltpu.SemaphoreType.DMA((3,)),
         ],
-    )(kv, got)
+    )(kv, got.reshape(cores, chips, height, LANES))
 
 
 def square(x):
@@ -231,13 +247,14 @@
 
 
 def merge_pair(halves, chips):
-    cores, height, _ = halves.shape
-    rows = height // (chips + 1)
-
-    def body(x_ref, out_ref):
+    cores = len(halves)
+    rows = halves[0].shape[0] // (chips + 1)
+
+    def body(*refs):
+        x_refs, out_ref = refs[:cores], refs[cores]
         logs = []
         for c in range(cores):
-            tail = x_ref[c, chips * rows :, :].astype(jnp.float32)
+            tail = x_refs[c][chips * rows :, :].astype(jnp.float32)
             logs.append(tail + pltpu.roll(tail, LANES - chips, 1) + pltpu.roll(tail, LANES - 2 * chips, 1))
         top = logs[0]
         for one in logs[1:]:
@@ -250,7 +267,7 @@
         sub = iota((8, LANES), 0)
         for d in range(chips):
             mixed = sum(
-                weight[c][:, d : d + 1] * x_ref[c, d * rows : (d + 1) * rows, :].astype(jnp.float32) for c in range(cores)
+                weight[c][:, d : d + 1] * x_refs[c][d * rows : (d + 1) * rows, :].astype(jnp.float32) for c in range(cores)
             )
             out_ref[d, :rows, :] = mixed.astype(jnp.bfloat16)
             tail = jnp.where(sub == 0, first[d : d + 1], jnp.where(sub == 1, second[d : d + 1], third[d : d + 1]))
@@ -261,10 +278,10 @@
         body,
         name="merge_pair",
         out_shape=jax.ShapeDtypeStruct((chips, rows + 8, LANES), jnp.bfloat16),
-        in_specs=[vmem],
+        in_specs=[vmem] * cores,
         out_specs=vmem,
         compiler_params=limit(4096),
-    )(halves)
+    )(*halves)
 
 
 def finish(got, requests):
@@ -310,12 +327,16 @@
     requests, q_heads, head_dim = queries.shape
     pool_dev, kv_heads, _, block_len, _ = kv_cache.shape
     assert kv_heads == 1
-    message = pack(queries, positions, keep, lengths, placement, chips, cores, pool_dev, block_len)
-    asked = lax.all_to_all(message, "dp", 0, 0, tiled=True)
+    near, far = NEAR, chips // NEAR
+    message = pack(queries, positions, keep, lengths, placement, chips, near, cores, pool_dev, block_len)
+    apart = [[j * near + p for j in range(far)] for p in range(near)]
+    beside = [[j * near + p for p in range(near)] for j in range(far)]
+    asked = lax.all_to_all(message, "dp", 0, 0, tiled=True, axis_index_groups=apart)
+    asked = lax.all_gather(asked, "dp", axis_index_groups=beside)
     asked = lax.all_gather(asked, "sub")
-    partials = attend(kv_cache.reshape(pool_dev, 2, block_len, head_dim), asked, requests)
-    halves = lax.all_to_all(partials, "sub", 0, 0, tiled=True)
-    answer = lax.all_to_all(merge_pair(halves, chips), "dp", 0, 0, tiled=True)
+    send, own = attend(kv_cache.reshape(pool_dev, 2, block_len, head_dim), asked, requests)
+    other = lax.ppermute(send, "sub", [(c, (c + 1) % cores) for c in range(cores)])
+    answer = lax.all_to_all(merge_pair((own, other), chips), "dp", 0, 0, tiled=True)
     return finish(answer, requests)
 
 

time: 106 us -> 101 us (0.953)
  blocking collectives: 95.2 us -> 89.4 us
  Pallas kernels: 9.45 us -> 7.14 us
  starting transfers between devices: 0 us -> 2.08 us
  waiting for transfers between devices: 0 us -> 1.4 us
    all_to_all x3 -> x2, blocking collectives: 93 us -> 81.3 us  [the longest x1 58.2 us: local(): lax.all_to_all(message, 'dp', 0, 0, tiled=True, axis_index_groups=apart)]
    all_gather x0 -> x1, blocking collectives: none -> 5.81 us  [local(): asked = lax.all_gather(asked, 'dp', axis_index_groups=beside)]
    pallas_call x2, Pallas kernels: 7.98 us -> 5.66 us  [the longest x1 3.78 us: attend(): pl.pallas_call(body, name='attend', out_shape=(half, half), in_specs=[pl....]
    ppermute x0 -> x1, starting transfers between devices: none -> 2.08 us  [local(): lax.ppermute(send, 'sub', [(c, (c + 1) % cores) for c in range(cores)])]
    ppermute x0 -> x1, waiting for transfers between devices: none -> 1.4 us  [local(): lax.ppermute(send, 'sub', [(c, (c + 1) % cores) for c in range(cores)])]
  transfers between devices with their start and end apart: 0 -> 1, of which waited for: 0 -> 1; matrix products, arithmetic and copies ran while one was open for 0% -> 0% of each run, Pallas kernels for 0% -> 0%
where the time goes in v3:
time: 101 us
  blocking collectives  89.4 us (89%)
  Pallas kernels  7.14 us (7%)
  starting transfers between devices  2.08 us (2%)
  waiting for transfers between devices  1.4 us (1%)
    all_to_all x1, blocking collectives, local(): lax.all_to_all(message, 'dp', 0, 0, tiled=True, axis_index_groups=apart)  58.2 us
    all_to_all x1, blocking collectives, local(): lax.all_to_all(merge_pair((own, other), chips), 'dp', 0, 0, tiled=True)  23 us
    all_gather x1, blocking collectives, local(): asked = lax.all_gather(asked, 'dp', axis_index_groups=beside)  5.81 us
    pallas_call x1, Pallas kernels, attend(): pl.pallas_call(body, name='attend', out_shape=(half, half), in_specs=[pl....  3.78 us
    all_gather x1, blocking collectives, local(): asked = lax.all_gather(asked, 'sub')  2.25 us
    ppermute x1, starting transfers between devices, local(): lax.ppermute(send, 'sub', [(c, (c + 1) % cores) for c in range(cores)])  2.08 us
  transfers between devices with their start and end apart: 1, of which 1 were waited for; matrix products, arithmetic and copies ran while one was open for 0% of the time, Pallas kernels for 0%

profile of v3, /device:TPU:80, one launch (start us, length us, event | category | flops | bytes accessed | tf_op | source)
XLA Modules:
  0.0 100.6 jit_solution(4792829529042495875)
XLA Ops:
  0.6 1.9 %pack.1 = bf16[8,72,128]{2,1,0:T(8,128)(2,1)} custom-call(s32[8]{0:T(128)} %lengths_ref.1, s32[8]{0:T(128)} %positions_ref.1, bf16[8,8,128]{2,1,0:T(8,128)(2,1)} %q_ref.1, f32[8,128]{1,0:T(8,128)} %constant.2.clone.freq_ref, s32[8,48]{1,0:T(8,128)} %keep_ref.1, s32[8,64]{1,0:T(8,128)} %place_ref.1), custom_call_target="tpu_custom_call" | custom-call | tf_op jit(solution)/shard_map/pack/pallas_call | solution.py:115
  2.5 58.2 %all_to_all.10 = bf16[8,72,128]{2,1,0:T(8,128)(2,1)S(1)} all-to-all(bf16[8,72,128]{2,1,0:T(8,128)(2,1)} %pack.1), channel_id=1, replica_groups={{0,32,64,96,128,160,192,224},{16,48,80,112,144,176,208,240},{1,33,65,97..., dimensions={0} | all-to-all | bytes 294912 | tf_op jit(solution)/shard_map/all_to_all | solution.py:334
  60.8 5.8 %all-gather = bf16[16,72,128]{2,1,0:T(8,128)(2,1)S(1)} all-gather(bf16[8,72,128]{2,1,0:T(8,128)(2,1)S(1)} %all_to_all.10), channel_id=2, replica_groups={{0,16},{32,48},{64,80},{96,112},{128,144},{160,176},{192,208},{224,240}..., dimensions={0}, use_global_device_ids=true | all-gather | bytes 442368 | tf_op jit(solution)/shard_map/all_gather | solution.py:335
  66.6 2.2 %all-gather.1 = bf16[4,8,72,128]{3,2,1,0:T(8,128)(2,1)S(1)} all-gather(bf16[2,8,72,128]{3,2,1,0:T(8,128)(2,1)S(1)} %bitcast.5), channel_id=3, replica_groups=mesh['groups'=2,'dp'=16,'head'=8,'sub'=2] {'sub'}, dimensions={0}, use_global_device_ids=true | all-gather | bytes 884736 | tf_op jit(solution)/shard_map/all_gather | solution.py:336
  68.8 3.8 %attend.1 = (bf16[1088,128]{1,0:T(8,128)(2,1)S(1)}, bf16[1088,128]{1,0:T(8,128)(2,1)S(1)}) custom-call(bf16[512,2,16,128]{3,2,1,0:T(8,128)(2,1)} %bitcast.4, bf16[2,16,72,128]{3,2,1,0:T(8,128)(2,1)S(1)} %bitcast.3), custom_call_target="tpu_custom_call" | custom-call | tf_op jit(solution)/shard_map/attend/pallas_call | solution.py:226
  72.6 2.1 %collective-permute-start = (bf16[1088,128]{1,0:T(8,128)(2,1)S(1)}, bf16[1088,128]{1,0:T(8,128)(2,1)S(1)}, u32[]{:S(2)}, u32[]{:S(2)}) collective-permute-start(bf16[1088,128]{1,0:T(8,128)(2,1)S(1)} %get-tuple-element.5), channel_id=1, source_target_pairs={{0,1},{1,0},{2,3},{3,2},{4,5},{5,4},{6,7},{7,6},{8,9},{9,8},{10,11... | collective-permute-start | bytes 835592 | tf_op jit(solution)/shard_map/ppermute | solution.py:338
  74.7 1.4 %collective-permute-done.refs_1_ = bf16[1088,128]{1,0:T(8,128)(2,1)S(1)} collective-permute-done((bf16[1088,128]{1,0:T(8,128)(2,1)S(1)}, bf16[1088,128]{1,0:T(8,128)(2,1)S(1)}, u32[]{:S(2)}, u32[]{:S(2)}) %collective-permute-start) | collective-permute-done | bytes 278560 | tf_op jit(solution)/shard_map/ppermute | solution.py:338
  76.1 0.5 merge_pair.1
  76.6 23.0 %all_to_all.11.x_ref = bf16[16,72,128]{2,1,0:T(8,128)(2,1)S(1)} all-to-all(bf16[16,72,128]{2,1,0:T(8,128)(2,1)S(1)} %merge_pair.1), channel_id=1, replica_groups=mesh['groups'=2,'dp'=16,'head'=8,'sub'=2] {'dp'}, dimensions={0} | all-to-all | bytes 589824 | tf_op jit(solution)/shard_map/all_to_all | solution.py:339
  99.6 1.0 finish.1
Async XLA Ops:
  72.6 3.5 %collective-permute-start = (bf16[1088,128]{1,0:T(8,128)(2,1)S(1)}, bf16[1088,128]{1,0:T(8,128)(2,1)S(1)}, u32[]{:S(2)}, u32[]{:S(2)}) collective-permute-start(bf16[1088,128]{1,0:T(8,128)(2,1)S(1)} %get-tuple-element.5), channel_id=1, source_target_pairs={{0,1},{1,0},{2,3},{3,2},{4,5},{5,4},{6,7},{7,6},{8,9},{9,8},{10,11... | collective-permute-start | bytes 835592 | tf_op jit(solution)/shard_map/ppermute | solution.py:338

commit v4 on v3

--- a/solution.py
+++ b/solution.py
@@ -10,7 +10,7 @@
 LOW = -1e30
 LOG2E = 1.4426950408889634
 NEAR = 2
-UNROLL = True
+CORES = 2
 PACK_LIMIT = 60 * 1024
 ATTEND_LIMIT = 52000
 
@@ -129,8 +129,21 @@
     return first, second, rest - second
 
 
+def abreast(x, width):
+    lane = iota(x.shape, 1)
+    first, second, third = pieces(x)
+    second, third = pltpu.roll(second, width, 1), pltpu.roll(third, 2 * width, 1)
+    return jnp.where(lane < width, first, jnp.where(lane < 2 * width, second, third)).astype(jnp.bfloat16)
+
+
+def together(x, width):
+    x = x.astype(jnp.float32)
+    return x + pltpu.roll(x, LANES - width, 1) + pltpu.roll(x, LANES - 2 * width, 1)
+
+
 def attend(kv, got, requests):
-    cores, near, far, height, _ = got.shape
+    members, far, height, _ = got.shape
+    near, cores = members // CORES, CORES
     pool_dev, _, block_len, _ = kv.shape
     chips = near * far
     rows = height - 8
@@ -139,7 +152,6 @@
     spread = LANES // (4 * cores)
     tokens = spread * block_len
     factor = LANES ** (-0.5) * LOG2E
-    assert cores == 2
 
     def body(kv_ref, got_ref, send_ref, keep_ref, k_ref, v_ref, ids_ref, live_ref, weight_ref, rows_ref, sems):
         k_copy = pltpu.make_async_copy(kv_ref.at[:, 0], k_ref, sems.at[0])
@@ -147,7 +159,7 @@
         k_copy.start()
         me = lax.axis_index("sub")
         at = me * spread
-        tails = jnp.concatenate([got_ref[s // chips, s % chips, rows:, :] for s in range(sources)], axis=0)
+        tails = jnp.concatenate([got_ref[s, rows:, :] for s in range(sources)], axis=0)
         mine_row = iota((sources, 8 * sources), 0) * 8 + lax.axis_index("dp") % near
         select = jnp.where(iota((sources, 8 * sources), 1) == mine_row, 1.0, 0.0).astype(jnp.bfloat16)
         meta = jnp.dot(select, tails, preferred_element_type=jnp.float32).astype(jnp.bfloat16)
@@ -177,18 +189,21 @@
         def held(ref, s):
             return jnp.concatenate([ref[rows_ref[s, k]] for k in range(spread)], axis=0)
 
-        def chip(i):
-            return (i & (far - 1)) * near + (i >> bits(far))
+        this = lax.axis_index("dp") % near
+
+        def source(c, t):
+            return (((this + 1 + t // far) % near) * cores + c) * far + t % far
 
         whose = (1 - me, me)
         peaks = []
         for c in whose:
 
-            def look(i, peak_of, c=c):
-                s = c * chips + i
+            peak_of = low
+            for t in range(chips):
+                s = source(c, t)
                 score = (
                     lax.dot_general(
-                        got_ref[c, i, :rows, :], held(k_ref, s), (((1,), (1,)), ((), ())), preferred_element_type=jnp.float32
+                        got_ref[s, :rows, :], held(k_ref, s), (((1,), (1,)), ((), ())), preferred_element_type=jnp.float32
                     )
                     * factor
                 )
@@ -196,37 +211,30 @@
                 score = jnp.where(mine, score, LOW)
                 peak = jnp.max(score, axis=1, keepdims=True)
                 weight_ref[s] = jnp.where(mine, jnp.exp2(score - peak), 0.0).astype(jnp.bfloat16)
-                return jnp.where(lane == chip(i), peak, peak_of)
-
-            peaks.append(lax.fori_loop(0, chips, look, low, unroll=UNROLL))
+                peak_of = jnp.where(lane == t, peak, peak_of)
+            peaks.append(peak_of)
         v_copy.wait()
         for c, peak_of, out_ref in zip(whose, peaks, (send_ref, keep_ref)):
-
-            def add(i, total_of, c=c, out_ref=out_ref):
-                s = c * chips + i
+            total_of = jnp.zeros((rows, LANES), jnp.float32)
+            for t in range(chips):
+                s = source(c, t)
                 vs = jnp.concatenate([held(v_ref, s), fill], axis=1)
                 both = jnp.dot(weight_ref[s], vs, preferred_element_type=jnp.float32)
                 total = both[:, LANES:]
                 safe = jnp.where(total > 0.0, total, 1.0)
-                start = pl.multiple_of(chip(i) * rows, rows)
-                out_ref[pl.ds(start, rows), :] = (both[:, :LANES] / safe).astype(jnp.bfloat16)
-                return jnp.where(lane == chip(i), total, total_of)
-
-            total = lax.fori_loop(0, chips, add, jnp.zeros((rows, LANES), jnp.float32), unroll=UNROLL)
-            some = total > 0.0
-            logs = peak_of * (1.0 / LOG2E) + jnp.log(jnp.where(some, total, 1.0))
-            first, second, third = pieces(jnp.where(some, logs, LOW))
-            second, third = pltpu.roll(second, chips, 1), pltpu.roll(third, 2 * chips, 1)
-            out_ref[chips * rows :, :] = jnp.where(
-                lane < chips, first, jnp.where(lane < 2 * chips, second, third)
-            ).astype(jnp.bfloat16)
+                out_ref[t * rows : (t + 1) * rows, :] = (both[:, :LANES] / safe).astype(out_ref.dtype)
+                total_of = jnp.where(lane == t, total, total_of)
+            some = total_of > 0.0
+            logs = peak_of * (1.0 / LOG2E) + jnp.log(jnp.where(some, total_of, 1.0))
+            logs = jnp.where(some, logs, LOW)
+            out_ref[chips * rows :, :] = logs if out_ref is keep_ref else abreast(logs, chips)
 
     vmem = pl.BlockSpec(memory_space=pltpu.VMEM)
-    half = jax.ShapeDtypeStruct((chips * rows + rows, LANES), jnp.bfloat16)
+    half = (chips * rows + rows, LANES)
     return pl.pallas_call(
         body,
         name="attend",
-        out_shape=(half, half),
+        out_shape=(jax.ShapeDtypeStruct(half, jnp.bfloat16), jax.ShapeDtypeStruct(half, jnp.float32)),
         in_specs=[pl.BlockSpec(memory_space=pltpu.HBM), vmem],
         out_specs=(vmem, vmem),
         compiler_params=limit(ATTEND_LIMIT),
@@ -239,49 +247,60 @@
             pltpu.SMEM((sources, LANES), jnp.int32),
             pltpu.SemaphoreType.DMA((3,)),
         ],
-    )(kv, got.reshape(cores, chips, height, LANES))
+    )(kv, got.reshape(sources, height, LANES))
 
 
 def square(x):
     return jnp.concatenate([x, jnp.zeros((LANES - x.shape[0], LANES), x.dtype)], axis=0).T
 
 
-def merge_pair(halves, chips):
-    cores = len(halves)
-    rows = halves[0].shape[0] // (chips + 1)
-
-    def body(*refs):
-        x_refs, out_ref = refs[:cores], refs[cores]
-        logs = []
-        for c in range(cores):
-            tail = x_refs[c][chips * rows :, :].astype(jnp.float32)
-            logs.append(tail + pltpu.roll(tail, LANES - chips, 1) + pltpu.roll(tail, LANES - 2 * chips, 1))
-        top = logs[0]
-        for one in logs[1:]:
-            top = jnp.maximum(top, one)
-        scale = [jnp.exp(one - top) for one in logs]
-        norm = sum(scale[1:], scale[0])
-        weight = [one / norm for one in scale]
-        whole = square(top + jnp.log(norm))[:chips]
-        first, second, third = pieces(whole)
+def merge(keep, got, axis, width, rows, last):
+    near = got.shape[0]
+    assert near == 2
+
+    def body(keep_ref, got_ref, *outs):
+        partner = near - 1 - lax.axis_index(axis) % near
+        mine = keep_ref[width * rows :, :]
+        other = together(got_ref[partner, width * rows :, :], width)
+        top = jnp.maximum(mine, other)
+        mine, other = jnp.exp(mine - top), jnp.exp(other - top)
+        norm = mine + other
+        mine, other = mine / norm, other / norm
+        logs = top + jnp.log(norm)
+
+        def mixed(d):
+            own = mine[:, d : d + 1] * keep_ref[d * rows : (d + 1) * rows, :]
+            return own + other[:, d : d + 1] * got_ref[partner, d * rows : (d + 1) * rows, :].astype(jnp.float32)
+
+        if not last:
+            part = width // 2
+            for d in range(part):
+                outs[0][d * rows : (d + 1) * rows, :] = mixed(d).astype(jnp.bfloat16)
+                outs[1][d * rows : (d + 1) * rows, :] = mixed(part + d)
+            outs[0][part * rows :, :] = abreast(logs, part)
+            outs[1][part * rows :, :] = pltpu.roll(logs, LANES - part, 1)
+            return
+        first, second, third = pieces(square(logs)[:width])
         sub = iota((8, LANES), 0)
-        for d in range(chips):
-            mixed = sum(
-                weight[c][:, d : d + 1] * x_refs[c][d * rows : (d + 1) * rows, :].astype(jnp.float32) for c in range(cores)
-            )
-            out_ref[d, :rows, :] = mixed.astype(jnp.bfloat16)
+        for d in range(width):
+            outs[0][d, :rows, :] = mixed(d).astype(jnp.bfloat16)
             tail = jnp.where(sub == 0, first[d : d + 1], jnp.where(sub == 1, second[d : d + 1], third[d : d + 1]))
-            out_ref[d, rows:, :] = tail.astype(jnp.bfloat16)
+            outs[0][d, rows:, :] = tail.astype(jnp.bfloat16)
 
     vmem = pl.BlockSpec(memory_space=pltpu.VMEM)
+    if last:
+        out_shape = (jax.ShapeDtypeStruct((width, rows + 8, LANES), jnp.bfloat16),)
+    else:
+        half = (width // 2 * rows + rows, LANES)
+        out_shape = (jax.ShapeDtypeStruct(half, jnp.bfloat16), jax.ShapeDtypeStruct(half, jnp.float32))
     return pl.pallas_call(
         body,
-        name="merge_pair",
-        out_shape=jax.ShapeDtypeStruct((chips, rows + 8, LANES), jnp.bfloat16),
-        in_specs=[vmem] * cores,
-        out_specs=vmem,
+        name="merge_" + axis,
+        out_shape=out_shape,
+        in_specs=[vmem, vmem],
+        out_specs=(vmem,) * len(out_shape),
         compiler_params=limit(4096),
-    )(*halves)
+    )(keep, got)
 
 
 def finish(got, requests):
@@ -326,17 +345,19 @@
     chips, cores = lax.axis_size("dp"), lax.axis_size("sub")
     requests, q_heads, head_dim = queries.shape
     pool_dev, kv_heads, _, block_len, _ = kv_cache.shape
-    assert kv_heads == 1
+    assert kv_heads == 1 and cores == CORES
     near, far = NEAR, chips // NEAR
     message = pack(queries, positions, keep, lengths, placement, chips, near, cores, pool_dev, block_len)
     apart = [[j * near + p for j in range(far)] for p in range(near)]
     beside = [[j * near + p for p in range(near)] for j in range(far)]
     asked = lax.all_to_all(message, "dp", 0, 0, tiled=True, axis_index_groups=apart)
-    asked = lax.all_gather(asked, "dp", axis_index_groups=beside)
-    asked = lax.all_gather(asked, "sub")
+    around = [[j * near * cores + m for m in range(near * cores)] for j in range(far)]
+    asked = lax.all_gather(asked, ("dp", "sub"), axis_index_groups=around)
+    rows = requests * q_heads
     send, own = attend(kv_cache.reshape(pool_dev, 2, block_len, head_dim), asked, requests)
-    other = lax.ppermute(send, "sub", [(c, (c + 1) % cores) for c in range(cores)])
-    answer = lax.all_to_all(merge_pair((own, other), chips), "dp", 0, 0, tiled=True)
+    send, own = merge(own, lax.all_gather(send, "sub"), "sub", chips, rows, False)
+    (answer,) = merge(own, lax.all_gather(send, "dp", axis_index_groups=beside), "dp", far, rows, True)
+    answer = lax.all_to_all(answer, "dp", 0, 0, tiled=True, axis_index_groups=apart)
     return finish(answer, requests)
 
 

time: 101 us -> 102 us (level)
  blocking collectives: 89.4 us -> 93.9 us
  starting transfers between devices: 2.08 us -> 0 us
  waiting for transfers between devices: 1.4 us -> 0 us
    all_gather x2 -> x3, blocking collectives: 8.06 us -> 16.4 us  [the longest x1 7.32 us: local(): asked = lax.all_gather(asked, ('dp', 'sub'), axis_index_groups=around)]
    all_to_all x1, blocking collectives: 23 us -> 19.3 us  [local(): lax.all_to_all(answer, 'dp', 0, 0, tiled=True, axis_index_groups=apart)]
    ppermute x1 -> x0, starting transfers between devices: 2.08 us -> none  [local(): lax.ppermute(send, 'sub', [(c, (c + 1) % cores) for c in range(cores)])]
    ppermute x1 -> x0, waiting for transfers between devices: 1.4 us -> none  [local(): lax.ppermute(send, 'sub', [(c, (c + 1) % cores) for c in range(cores)])]
    pallas_call x2 -> x3, Pallas kernels: 4.27 us -> 4.52 us  [the longest x1 3.72 us: attend(): pl.pallas_call(body, name='attend', out_shape=(jax.ShapeDtypeStruct(half,...]
  transfers between devices with their start and end apart: 1 -> 0, of which waited for: 1 -> 0; matrix products, arithmetic and copies ran while one was open for 0% -> 0% of each run, Pallas kernels for 0% -> 0%
where the time goes in v4:
time: 102 us
  blocking collectives  93.9 us (92%)
  Pallas kernels  7.29 us (7%)
    all_to_all x1, blocking collectives, local(): lax.all_to_all(message, 'dp', 0, 0, tiled=True, axis_index_groups=apart)  58.2 us
    all_to_all x1, blocking collectives, local(): lax.all_to_all(answer, 'dp', 0, 0, tiled=True, axis_index_groups=apart)  19.3 us
    all_gather x1, blocking collectives, local(): asked = lax.all_gather(asked, ('dp', 'sub'), axis_index_groups=around)  7.32 us
    all_gather x1, blocking collectives, local(): lax.all_gather(send, 'dp', axis_index_groups=beside)  6.8 us
    pallas_call x1, Pallas kernels, attend(): pl.pallas_call(body, name='attend', out_shape=(jax.ShapeDtypeStruct(half,...  3.72 us
    all_gather x1, blocking collectives, local(): lax.all_gather(send, 'sub')  2.26 us

profile of v4, /device:TPU:80, one launch (start us, length us, event | category | flops | bytes accessed | tf_op | source)
XLA Modules:
  0.0 101.8 jit_solution(9722491257601618419)
XLA Ops:
  0.6 1.9 %pack.1 = bf16[8,72,128]{2,1,0:T(8,128)(2,1)} custom-call(s32[8]{0:T(128)} %lengths_ref.1, s32[8]{0:T(128)} %positions_ref.1, bf16[8,8,128]{2,1,0:T(8,128)(2,1)} %q_ref.1, f32[8,128]{1,0:T(8,128)} %constant.2.clone.freq_ref, s32[8,48]{1,0:T(8,128)} %keep_ref.1, s32[8,64]{1,0:T(8,128)} %place_ref.1), custom_call_target="tpu_custom_call" | custom-call | tf_op jit(solution)/shard_map/pack/pallas_call | solution.py:115
  2.5 58.2 %all_to_all.10 = bf16[8,72,128]{2,1,0:T(8,128)(2,1)S(1)} all-to-all(bf16[8,72,128]{2,1,0:T(8,128)(2,1)} %pack.1), channel_id=1, replica_groups={{0,32,64,96,128,160,192,224},{16,48,80,112,144,176,208,240},{1,33,65,97..., dimensions={0} | all-to-all | bytes 294912 | tf_op jit(solution)/shard_map/all_to_all | solution.py:353
  60.8 7.3 %all-gather.got_ref = bf16[32,72,128]{2,1,0:T(8,128)(2,1)S(1)} all-gather(bf16[8,72,128]{2,1,0:T(8,128)(2,1)S(1)} %all_to_all.10), channel_id=2, replica_groups={{0,1,16,17},{32,33,48,49},{64,65,80,81},{96,97,112,113},{128,129,144,14..., dimensions={0}, use_global_device_ids=true | all-gather | bytes 737280 | tf_op jit(solution)/shard_map/all_gather | solution.py:355
  68.1 3.7 %attend.1 = (bf16[1088,128]{1,0:T(8,128)(2,1)S(1)}, f32[1088,128]{1,0:T(8,128)S(1)}) custom-call(bf16[512,2,16,128]{3,2,1,0:T(8,128)(2,1)} %bitcast.5, bf16[32,72,128]{2,1,0:T(8,128)(2,1)S(1)} %all-gather.got_ref), custom_call_target="tpu_custom_call" | custom-call | tf_op jit(solution)/shard_map/attend/pallas_call | solution.py:234
  71.8 2.3 %all-gather.1 = bf16[2176,128]{1,0:T(8,128)(2,1)S(1)} all-gather(bf16[1088,128]{1,0:T(8,128)(2,1)S(1)} %get-tuple-element.7), channel_id=3, replica_groups=mesh['groups'=2,'dp'=16,'head'=8,'sub'=2] {'sub'}, dimensions={0}, use_global_device_ids=true | all-gather | bytes 835584 | tf_op jit(solution)/shard_map/all_gather | solution.py:358
  74.1 0.5 merge_sub.1
  74.5 6.8 %all-gather.2 = bf16[1152,128]{1,0:T(8,128)(2,1)S(1)} all-gather(bf16[576,128]{1,0:T(8,128)(2,1)S(1)} %get-tuple-element.9), channel_id=4, replica_groups={{0,16},{32,48},{64,80},{96,112},{128,144},{160,176},{192,208},{224,240}..., dimensions={0}, use_global_device_ids=true | all-gather | bytes 442368 | tf_op jit(solution)/shard_map/all_gather | solution.py:359
  81.3 0.3 merge_dp.1
  81.7 19.3 %all_to_all.11.x_ref = bf16[8,72,128]{2,1,0:T(8,128)(2,1)S(1)} all-to-all(bf16[8,72,128]{2,1,0:T(8,128)(2,1)S(1)} %merge_dp.1), channel_id=1, replica_groups={{0,32,64,96,128,160,192,224},{16,48,80,112,144,176,208,240},{1,33,65,97..., dimensions={0} | all-to-all | bytes 294912 | tf_op jit(solution)/shard_map/all_to_all | solution.py:360
  101.0 0.9 finish.1

commit v5 on v4

--- a/solution.py
+++ b/solution.py
@@ -189,10 +189,9 @@
         def held(ref, s):
             return jnp.concatenate([ref[rows_ref[s, k]] for k in range(spread)], axis=0)
 
-        this = lax.axis_index("dp") % near
 
         def source(c, t):
-            return (((this + 1 + t // far) % near) * cores + c) * far + t % far
+            return ((t % near) * cores + c) * far + t // near
 
         whose = (1 - me, me)
         peaks = []
@@ -254,51 +253,35 @@
     return jnp.concatenate([x, jnp.zeros((LANES - x.shape[0], LANES), x.dtype)], axis=0).T
 
 
-def merge(keep, got, axis, width, rows, last):
-    near = got.shape[0]
-    assert near == 2
-
-    def body(keep_ref, got_ref, *outs):
-        partner = near - 1 - lax.axis_index(axis) % near
-        mine = keep_ref[width * rows :, :]
-        other = together(got_ref[partner, width * rows :, :], width)
+def merge(keep, got, rows):
+    cores = got.shape[0]
+    chips = keep.shape[0] // rows - 1
+    assert cores == 2
+
+    def body(keep_ref, got_ref, out_ref):
+        partner = cores - 1 - lax.axis_index("sub")
+        mine = keep_ref[chips * rows :, :]
+        other = together(got_ref[partner, chips * rows :, :], chips)
         top = jnp.maximum(mine, other)
         mine, other = jnp.exp(mine - top), jnp.exp(other - top)
         norm = mine + other
         mine, other = mine / norm, other / norm
-        logs = top + jnp.log(norm)
-
-        def mixed(d):
-            own = mine[:, d : d + 1] * keep_ref[d * rows : (d + 1) * rows, :]
-            return own + other[:, d : d + 1] * got_ref[partner, d * rows : (d + 1) * rows, :].astype(jnp.float32)
-
-        if not last:
-            part = width // 2
-            for d in range(part):
-                outs[0][d * rows : (d + 1) * rows, :] = mixed(d).astype(jnp.bfloat16)
-                outs[1][d * rows : (d + 1) * rows, :] = mixed(part + d)
-            outs[0][part * rows :, :] = abreast(logs, part)
-            outs[1][part * rows :, :] = pltpu.roll(logs, LANES - part, 1)
-            return
-        first, second, third = pieces(square(logs)[:width])
+        first, second, third = pieces(square(top + jnp.log(norm))[:chips])
         sub = iota((8, LANES), 0)
-        for d in range(width):
-            outs[0][d, :rows, :] = mixed(d).astype(jnp.bfloat16)
+        for d in range(chips):
+            at = slice(d * rows, (d + 1) * rows)
+            mixed = mine[:, d : d + 1] * keep_ref[at, :] + other[:, d : d + 1] * got_ref[partner, at, :].astype(jnp.float32)
+            out_ref[d, :rows, :] = mixed.astype(jnp.bfloat16)
             tail = jnp.where(sub == 0, first[d : d + 1], jnp.where(sub == 1, second[d : d + 1], third[d : d + 1]))
-            outs[0][d, rows:, :] = tail.astype(jnp.bfloat16)
+            out_ref[d, rows:, :] = tail.astype(jnp.bfloat16)
 
     vmem = pl.BlockSpec(memory_space=pltpu.VMEM)
-    if last:
-        out_shape = (jax.ShapeDtypeStruct((width, rows + 8, LANES), jnp.bfloat16),)
-    else:
-        half = (width // 2 * rows + rows, LANES)
-        out_shape = (jax.ShapeDtypeStruct(half, jnp.bfloat16), jax.ShapeDtypeStruct(half, jnp.float32))
     return pl.pallas_call(
         body,
-        name="merge_" + axis,
-        out_shape=out_shape,
+        name="merge",
+        out_shape=jax.ShapeDtypeStruct((chips, rows + 8, LANES), jnp.bfloat16),
         in_specs=[vmem, vmem],
-        out_specs=(vmem,) * len(out_shape),
+        out_specs=vmem,
         compiler_params=limit(4096),
     )(keep, got)
 
@@ -349,15 +332,13 @@
     near, far = NEAR, chips // NEAR
     message = pack(queries, positions, keep, lengths, placement, chips, near, cores, pool_dev, block_len)
     apart = [[j * near + p for j in range(far)] for p in range(near)]
-    beside = [[j * near + p for p in range(near)] for j in range(far)]
     asked = lax.all_to_all(message, "dp", 0, 0, tiled=True, axis_index_groups=apart)
     around = [[j * near * cores + m for m in range(near * cores)] for j in range(far)]
     asked = lax.all_gather(asked, ("dp", "sub"), axis_index_groups=around)
     rows = requests * q_heads
     send, own = attend(kv_cache.reshape(pool_dev, 2, block_len, head_dim), asked, requests)
-    send, own = merge(own, lax.all_gather(send, "sub"), "sub", chips, rows, False)
-    (answer,) = merge(own, lax.all_gather(send, "dp", axis_index_groups=beside), "dp", far, rows, True)
-    answer = lax.all_to_all(answer, "dp", 0, 0, tiled=True, axis_index_groups=apart)
+    answer = merge(own, lax.all_gather(send, "sub"), rows)
+    answer = lax.all_to_all(answer, "dp", 0, 0, tiled=True)
     return finish(answer, requests)
 
 

time: 102 us -> 99.3 us (0.974)
  blocking collectives: 93.9 us -> 91.3 us
    all_gather x2 -> x1, blocking collectives: 9.06 us -> 2.26 us  [local(): answer = merge(own, lax.all_gather(send, 'sub'), rows)]
    all_to_all x1, blocking collectives: 19.3 us -> 23.5 us  [local(): answer = lax.all_to_all(answer, 'dp', 0, 0, tiled=True)]
where the time goes in v5:
time: 99.3 us; the launch traced here: 99 us
  blocking collectives  91.3 us (92%)
  Pallas kernels  7.06 us (7%)
    all_to_all x1, blocking collectives, local(): lax.all_to_all(message, 'dp', 0, 0, tiled=True, axis_index_groups=apart)  58.2 us
    all_to_all x1, blocking collectives, local(): answer = lax.all_to_all(answer, 'dp', 0, 0, tiled=True)  23.5 us
    all_gather x1, blocking collectives, local(): asked = lax.all_gather(asked, ('dp', 'sub'), axis_index_groups=around)  7.32 us
    pallas_call x1, Pallas kernels, attend(): pl.pallas_call(body, name='attend', out_shape=(jax.ShapeDtypeStruct(half,...  3.71 us
    all_gather x1, blocking collectives, local(): answer = merge(own, lax.all_gather(send, 'sub'), rows)  2.26 us

profile of v5, /device:TPU:80, one launch (start us, length us, event | category | flops | bytes accessed | tf_op | source)
XLA Modules:
  0.0 99.0 jit_solution(3199175585085063409)
XLA Ops:
  0.6 1.9 %pack.1 = bf16[8,72,128]{2,1,0:T(8,128)(2,1)} custom-call(s32[8]{0:T(128)} %lengths_ref.1, s32[8]{0:T(128)} %positions_ref.1, bf16[8,8,128]{2,1,0:T(8,128)(2,1)} %q_ref.1, f32[8,128]{1,0:T(8,128)} %constant.2.clone.freq_ref, s32[8,48]{1,0:T(8,128)} %keep_ref.1, s32[8,64]{1,0:T(8,128)} %place_ref.1), custom_call_target="tpu_custom_call" | custom-call | tf_op jit(solution)/shard_map/pack/pallas_call | solution.py:115
  2.5 58.2 %all_to_all.10 = bf16[8,72,128]{2,1,0:T(8,128)(2,1)S(1)} all-to-all(bf16[8,72,128]{2,1,0:T(8,128)(2,1)} %pack.1), channel_id=1, replica_groups={{0,32,64,96,128,160,192,224},{16,48,80,112,144,176,208,240},{1,33,65,97..., dimensions={0} | all-to-all | bytes 294912 | tf_op jit(solution)/shard_map/all_to_all | solution.py:335
  60.8 7.3 %all-gather.got_ref = bf16[32,72,128]{2,1,0:T(8,128)(2,1)S(1)} all-gather(bf16[8,72,128]{2,1,0:T(8,128)(2,1)S(1)} %all_to_all.10), channel_id=2, replica_groups={{0,1,16,17},{32,33,48,49},{64,65,80,81},{96,97,112,113},{128,129,144,14..., dimensions={0}, use_global_device_ids=true | all-gather | bytes 737280 | tf_op jit(solution)/shard_map/all_gather | solution.py:337
  68.1 3.7 %attend.1 = (bf16[1088,128]{1,0:T(8,128)(2,1)S(1)}, f32[1088,128]{1,0:T(8,128)S(1)}) custom-call(bf16[512,2,16,128]{3,2,1,0:T(8,128)(2,1)} %bitcast.3, bf16[32,72,128]{2,1,0:T(8,128)(2,1)S(1)} %all-gather.got_ref), custom_call_target="tpu_custom_call" | custom-call | tf_op jit(solution)/shard_map/attend/pallas_call | solution.py:233
  71.8 2.3 %all-gather.1 = bf16[2176,128]{1,0:T(8,128)(2,1)S(1)} all-gather(bf16[1088,128]{1,0:T(8,128)(2,1)S(1)} %get-tuple-element.5), channel_id=3, replica_groups=mesh['groups'=2,'dp'=16,'head'=8,'sub'=2] {'sub'}, dimensions={0}, use_global_device_ids=true | all-gather | bytes 835584 | tf_op jit(solution)/shard_map/all_gather | solution.py:340
  74.1 0.5 merge.1
  74.5 23.5 %all_to_all.11.x_ref = bf16[16,72,128]{2,1,0:T(8,128)(2,1)S(1)} all-to-all(bf16[16,72,128]{2,1,0:T(8,128)(2,1)S(1)} %merge.1), channel_id=1, replica_groups=mesh['groups'=2,'dp'=16,'head'=8,'sub'=2] {'dp'}, dimensions={0} | all-to-all | bytes 589824 | tf_op jit(solution)/shard_map/all_to_all | solution.py:341
  98.0 1.0 %finish.1 = (bf16[8,8,128]{2,1,0:T(8,128)(2,1)}, f32[8,8]{1,0:T(8,128)}) custom-call(bf16[16,72,128]{2,1,0:T(8,128)(2,1)S(1)} %all_to_all.11.x_ref), custom_call_target="tpu_custom_call" | custom-call | tf_op jit(solution)/shard_map/finish/pallas_call | solution.py:314
